TPU v7x, 32 devices: a 4x4x1 block of a 4x4x8 slice. The times are simulated.
32 devices in a mesh: inst: 1 (over z), qy: 4 (over y), qx: 8 (over x, core).
Axes of the slice: x: 4, y: 4, z: 1, core: 2. Of those that a mesh axis runs over, the one named last changes fastest.
The devices are a block of a 4x4x8 slice.
Arguments:
- cost: float32 [2097152], P(('inst', 'qy', 'qx'))
- gamma: float32 [2, 3], P('inst')
- beta: float32 [2, 3], P('inst')
Outputs:
- output 1: float32 [2], P('inst')
- output 2: float32 [2, 6], P('inst')
All inputs are finite; a program needn't handle non-finite values.
Results may differ from a plain program's by a relative error of at most 0.001.
Values sent between devices are 32-bit elements.
A program may use at most 768 MiB of HBM per device.

v0:
```python
import jax
import jax.numpy as jnp
from jax import lax
from jax.sharding import PartitionSpec as P

LANE_BITS = 7
LANE_WIDTH = 128


def flip_grid(amplitudes, qubit):
    if qubit < LANE_BITS:
        shift = 2 ** qubit
        position = lax.broadcasted_iota(jnp.int32, (LANE_WIDTH,), 0)
        axis_pos = amplitudes.ndim - 1
    else:
        shift = 2 ** (qubit - LANE_BITS)
        position = lax.broadcasted_iota(jnp.int32, (amplitudes.shape[-2], 1), 0)
        axis_pos = amplitudes.ndim - 2
    upper = (position & shift) != 0
    return jnp.where(upper, jnp.roll(amplitudes, shift, axis=axis_pos), jnp.roll(amplitudes, -shift, axis=axis_pos))


def partner_tables(mesh):
    tables = []
    for axis_name in ('qx', 'qy'):
        width = mesh.shape[axis_name]
        for bit_pos in range(width.bit_length() - 1):
            tables.append((axis_name, [(index, index ^ (1 << bit_pos)) for index in range(width)]))
    return tables


def inverse_step(four_amps, partner, cos_b, sin_b):
    psi_re, psi_im, lam_re, lam_im = four_amps
    term = jnp.sum(lam_re * partner[1] - lam_im * partner[0], axis=(1, 2))
    updated = (cos_b * psi_re - sin_b * partner[1], cos_b * psi_im + sin_b * partner[0], cos_b * lam_re - sin_b * partner[3], cos_b * lam_im + sin_b * partner[2])
    return updated, term


def solution(mesh):
    partners = partner_tables(mesh)
    global_count = len(partners)
    group_axes = ('qy', 'qx')

    def device_fn(cost, gamma, beta):
        local_size = cost.shape[0]
        local_count = local_size.bit_length() - 1
        row_count = local_size // LANE_WIDTH
        num_sets, num_layers = gamma.shape
        start_amp = 2.0 ** (-0.5 * (local_count + global_count))
        cost_grid = cost.reshape(1, row_count, LANE_WIDTH)
        gamma_grid = gamma[:, :, None, None]
        half_cos = jnp.cos(0.5 * beta)[:, :, None, None]
        half_sin = jnp.sin(0.5 * beta)[:, :, None, None]
        psi_re = jnp.full((num_sets, row_count, LANE_WIDTH), start_amp, jnp.float32)
        psi_im = jnp.zeros_like(psi_re)
        phase_saved = []
        for layer in range(num_layers):
            phase = gamma_grid[:, layer] * cost_grid
            cos_p = jnp.cos(phase)
            sin_p = jnp.sin(phase)
            phase_saved.append((cos_p, sin_p))
            psi_re, psi_im = psi_re * cos_p + psi_im * sin_p, psi_im * cos_p - psi_re * sin_p
            cos_b = half_cos[:, layer]
            sin_b = half_sin[:, layer]
            for qubit in range(local_count):
                flip_re = flip_grid(psi_re, qubit)
                flip_im = flip_grid(psi_im, qubit)
                psi_re, psi_im = cos_b * psi_re + sin_b * flip_im, cos_b * psi_im - sin_b * flip_re
            for axis_name, pair_list in partners:
                partner = lax.ppermute(jnp.stack([psi_re, psi_im]), axis_name, pair_list)
                psi_re, psi_im = cos_b * psi_re + sin_b * partner[1], cos_b * psi_im - sin_b * partner[0]
        energy_part = jnp.sum(cost_grid * (psi_re * psi_re + psi_im * psi_im), axis=(1, 2))
        four_amps = (psi_re, psi_im, cost_grid * psi_re, cost_grid * psi_im)
        gamma_grads = [None] * num_layers
        beta_grads = [None] * num_layers
        for layer in reversed(range(num_layers)):
            cos_b = half_cos[:, layer]
            sin_b = half_sin[:, layer]
            beta_term = jnp.zeros((num_sets,), jnp.float32)
            for qubit in range(local_count):
                flips = [flip_grid(amplitudes, qubit) for amplitudes in four_amps]
                four_amps, term = inverse_step(four_amps, flips, cos_b, sin_b)
                beta_term = beta_term + term
            for axis_name, pair_list in partners:
                partner = lax.ppermute(jnp.stack(list(four_amps)), axis_name, pair_list)
                four_amps, term = inverse_step(four_amps, partner, cos_b, sin_b)
                beta_term = beta_term + term
            psi_re, psi_im, lam_re, lam_im = four_amps
            beta_grads[layer] = beta_term
            gamma_grads[layer] = 2.0 * jnp.sum(cost_grid * (lam_re * psi_im - lam_im * psi_re), axis=(1, 2))
            if layer > 0:
                cos_p, sin_p = phase_saved[layer]
                four_amps = (psi_re * cos_p - psi_im * sin_p, psi_im * cos_p + psi_re * sin_p, lam_re * cos_p - lam_im * sin_p, lam_im * cos_p + lam_re * sin_p)
        grad_rows = jnp.stack(gamma_grads + beta_grads, axis=1)
        totals = lax.psum(jnp.concatenate([energy_part[:, None], grad_rows], axis=1), group_axes)
        return totals[:, 0], totals[:, 1:]

    cost_spec = P(('inst', 'qy', 'qx'))
    angle_spec = P('inst', None)
    return jax.shard_map(device_fn, mesh=mesh, in_specs=(cost_spec, angle_spec, angle_spec), out_specs=(P('inst'), angle_spec), check_vma=False)
```

profile of v0, /device:TPU:97, one launch (start us, length us, event | category | flops | bytes accessed | tf_op | source)
XLA Modules:
  0.0 1743.8 jit_solution(4868865576173577181)
XLA Ops:
  2.5 9.2 fusion.33
  18.2 10.1 fusion.129
  34.2 11.6 fusion.135
  103.4 4.0 fusion.159
  111.7 5.4 fusion.165
  121.4 5.5 fusion.167
  131.1 5.6 fusion.173
  141.0 5.3 fusion.175
  150.6 5.1 fusion.181
  160.1 7.9 fusion.183
  174.3 4.6 fusion.185
  181.0 45.7 %fusion.223 = f32[1,2,512,128]{3,1,2,0:T(2,128)S(1)} fusion(f32[1,2,384,128]{3,1,2,0:T(2,128)} %get-tuple-element.1804, f32[1,2,128,128]{3,1,2,0:T(2,128)} %get-tuple-element.1808, f32[1,2,128,128]{3,1,2,0:T(2,128)} %get-tuple-element.1807, f32[1,2,384,128]{3,1,2,0:T(2,128)} %get-tuple-element.1803, f32[1,2,256,128]{3,1,2,0:T(2,128)S(1)} %get-tuple-element.1685, ...), kind=kLoop, calls=%fused_computation.375 | loop fusion | flops 12582912 | bytes 16519960 | tf_op jit(solution)/shard_map/add | solution.py:68
  227.0 41.3 %fusion.258 = f32[1,2,512,128]{3,1,2,0:T(2,128)S(1)} fusion(f32[1,2,384,128]{3,1,2,0:T(2,128)} %get-tuple-element.1798, f32[1,2,128,128]{3,1,2,0:T(2,128)S(1)} %get-tuple-element.1800, f32[1,2,128,128]{3,1,2,0:T(2,128)} %get-tuple-element.1801, f32[1,2,384,128]{3,1,2,0:T(2,128)} %get-tuple-element.1796, f32[1,2,256,128]{3,1,2,0:T(2,128)S(1)} %get-tuple-element.1689, ...), kind=kLoop, calls=%fused_computation.426 | loop fusion | flops 12582912 | bytes 16519960 | tf_op jit(solution)/shard_map/sub | solution.py:68
  275.1 23.6 %collective-permute-done.1 = f32[2,2,512,128]{3,1,2,0:T(2,128)S(1)} collective-permute-done((f32[2,2,512,128]{3,1,2,0:T(2,128)S(1)}, f32[2,2,512,128]{3,1,2,0:T(2,128)S(1)}, u32[]{:S(2)}, u32[]{:S(2)}) %collective-permute-start.1) | collective-permute-done | bytes 1048608 | tf_op jit(solution)/shard_map/ppermute | solution.py:70
  302.2 22.6 %collective-permute-done.2 = f32[2,2,512,128]{3,1,2,0:T(2,128)S(1)} collective-permute-done((f32[2,2,512,128]{3,1,2,0:T(2,128)S(1)}, f32[2,2,512,128]{3,1,2,0:T(2,128)S(1)}, u32[]{:S(2)}, u32[]{:S(2)}) %collective-permute-start.2) | collective-permute-done | bytes 1048608 | tf_op jit(solution)/shard_map/ppermute | solution.py:70
  327.4 21.0 %collective-permute-done.3 = f32[2,2,512,128]{3,1,2,0:T(2,128)S(1)} collective-permute-done((f32[2,2,512,128]{3,1,2,0:T(2,128)S(1)}, f32[2,2,512,128]{3,1,2,0:T(2,128)S(1)}, u32[]{:S(2)}, u32[]{:S(2)}) %collective-permute-start.3) | collective-permute-done | bytes 1048608 | tf_op jit(solution)/shard_map/ppermute | solution.py:70
  353.4 4.5 multiply_cosine_fusion
  357.9 16.3 collective-permute-done.4
  374.2 5.3 multiply_add_fusion.66
  457.1 4.0 fusion.295
  465.4 5.1 broadcast_multiply_fusion
  474.8 5.6 broadcast_multiply_fusion.1
  484.7 5.4 fusion.300
  499.9 5.4 fusion.311
  507.4 4.5 fusion.316
  526.3 4.6 fusion.315
  531.7 5.5 maximum_multiply_fusion.12
  537.5 9.1 fusion.357
  547.0 29.8 %fusion.347 = (f32[1,2,512,128]{3,1,2,0:T(2,128)S(1)}, f32[1,2,512,128]{3,1,2,0:T(2,128)S(1)}) fusion(f32[1,2,496,128]{3,1,2,0:T(2,128)} %get-tuple-element.1556, f32[1,2,16,128]{3,1,2,0:T(2,128)S(1)} %copy-done.306, f32[1,2,16,128]{3,1,2,0:T(2,128)S(1)} %copy-done.305, f32[1,2,496,128]{3,1,2,0:T(2,128)} %get-tuple-element.1555, ...), kind=kLoop, calls=%fused_computation.560 | loop fusion | flops 10223616 | bytes 14945576 | tf_op jit(solution)/shard_map/mul | solution.py:68
  577.8 15.2 broadcast_multiply_fusion.3
  597.8 4.0 fusion.361
  614.2 23.1 %collective-permute-done.6 = f32[2,2,512,128]{3,1,2,0:T(2,128)S(1)} collective-permute-done((f32[2,2,512,128]{3,1,2,0:T(2,128)S(1)}, f32[2,2,512,128]{3,1,2,0:T(2,128)S(1)}, u32[]{:S(2)}, u32[]{:S(2)}) %collective-permute-start.6) | collective-permute-done | bytes 1048608 | tf_op jit(solution)/shard_map/ppermute | solution.py:70
  642.3 22.1 %collective-permute-done.7 = f32[2,2,512,128]{3,1,2,0:T(2,128)S(1)} collective-permute-done((f32[2,2,512,128]{3,1,2,0:T(2,128)S(1)}, f32[2,2,512,128]{3,1,2,0:T(2,128)S(1)}, u32[]{:S(2)}, u32[]{:S(2)}) %collective-permute-start.7) | collective-permute-done | bytes 1048608 | tf_op jit(solution)/shard_map/ppermute | solution.py:70
  665.8 21.8 %collective-permute-done.8 = f32[2,2,512,128]{3,2,1,0:T(8,128)S(1)} collective-permute-done((f32[2,2,512,128]{3,2,1,0:T(8,128)S(1)}, f32[2,2,512,128]{3,2,1,0:T(8,128)S(1)}, u32[]{:S(2)}, u32[]{:S(2)}) %collective-permute-start.8) | collective-permute-done | bytes 1048608 | tf_op jit(solution)/shard_map/ppermute | solution.py:70
  692.0 20.2 %collective-permute-done.9 = f32[2,2,512,128]{3,1,2,0:T(2,128)S(1)} collective-permute-done((f32[2,2,512,128]{3,1,2,0:T(2,128)S(1)}, f32[2,2,512,128]{3,1,2,0:T(2,128)S(1)}, u32[]{:S(2)}, u32[]{:S(2)}) %collective-permute-start.9) | collective-permute-done | bytes 1048608 | tf_op jit(solution)/shard_map/ppermute | solution.py:70
  713.3 4.7 copy_multiply_fusion.8
  738.2 4.1 fusion.382
  824.2 6.2 fusion.437
  830.7 5.5 fusion.439
  836.5 5.5 fusion.441
  842.2 6.5 fusion.496
  848.9 8.2 copy_multiply_fusion.1
  857.5 5.9 fusion.466
  863.5 4.4 collective-permute-start.10
  871.8 23.1 %collective-permute-done.11 = f32[2,2,512,128]{3,2,1,0:T(8,128)S(1)} collective-permute-done((f32[2,2,512,128]{3,2,1,0:T(8,128)S(1)}, f32[2,2,512,128]{3,2,1,0:T(8,128)S(1)}, u32[]{:S(2)}, u32[]{:S(2)}) %collective-permute-start.11) | collective-permute-done | bytes 1048608 | tf_op jit(solution)/shard_map/ppermute | solution.py:70
  898.3 22.1 %collective-permute-done.12 = f32[2,2,512,128]{3,2,1,0:T(8,128)S(1)} collective-permute-done((f32[2,2,512,128]{3,2,1,0:T(8,128)S(1)}, f32[2,2,512,128]{3,2,1,0:T(8,128)S(1)}, u32[]{:S(2)}, u32[]{:S(2)}) %collective-permute-start.12) | collective-permute-done | bytes 1048608 | tf_op jit(solution)/shard_map/ppermute | solution.py:70
  921.7 21.8 %collective-permute-done.13 = f32[2,2,512,128]{3,2,1,0:T(8,128)S(1)} collective-permute-done((f32[2,2,512,128]{3,2,1,0:T(8,128)S(1)}, f32[2,2,512,128]{3,2,1,0:T(8,128)S(1)}, u32[]{:S(2)}, u32[]{:S(2)}) %collective-permute-start.13) | collective-permute-done | bytes 1048608 | tf_op jit(solution)/shard_map/ppermute | solution.py:70
  946.7 22.0 %collective-permute-done.14 = f32[2,2,512,128]{3,2,1,0:T(8,128)S(1)} collective-permute-done((f32[2,2,512,128]{3,2,1,0:T(8,128)S(1)}, f32[2,2,512,128]{3,2,1,0:T(8,128)S(1)}, u32[]{:S(2)}, u32[]{:S(2)}) %collective-permute-start.14) | collective-permute-done | bytes 1048608 | tf_op jit(solution)/shard_map/ppermute | solution.py:70
  1020.1 45.7 %collective-permute-done.16 = f32[4,2,512,128]{3,2,1,0:T(8,128)S(1)} collective-permute-done((f32[4,2,512,128]{3,2,1,0:T(8,128)S(1)}, f32[4,2,512,128]{3,2,1,0:T(8,128)S(1)}, u32[]{:S(2)}, u32[]{:S(2)}) %collective-permute-start.16) | collective-permute-done | bytes 2097184 | tf_op jit(solution)/shard_map/ppermute | solution.py:85
  1070.0 44.6 %collective-permute-done.17 = f32[4,2,512,128]{3,2,1,0:T(8,128)S(1)} collective-permute-done((f32[4,2,512,128]{3,2,1,0:T(8,128)S(1)}, f32[4,2,512,128]{3,2,1,0:T(8,128)S(1)}, u32[]{:S(2)}, u32[]{:S(2)}) %collective-permute-start.17) | collective-permute-done | bytes 2097184 | tf_op jit(solution)/shard_map/ppermute | solution.py:85
  1115.9 44.8 %collective-permute-done.18 = f32[4,2,512,128]{3,2,1,0:T(8,128)S(1)} collective-permute-done((f32[4,2,512,128]{3,2,1,0:T(8,128)S(1)}, f32[4,2,512,128]{3,2,1,0:T(8,128)S(1)}, u32[]{:S(2)}, u32[]{:S(2)}) %collective-permute-start.18) | collective-permute-done | bytes 2097184 | tf_op jit(solution)/shard_map/ppermute | solution.py:85
  1164.0 43.6 %collective-permute-done.19 = f32[4,2,512,128]{3,2,1,0:T(8,128)S(1)} collective-permute-done((f32[4,2,512,128]{3,2,1,0:T(8,128)S(1)}, f32[4,2,512,128]{3,2,1,0:T(8,128)S(1)}, u32[]{:S(2)}, u32[]{:S(2)}) %collective-permute-start.19) | collective-permute-done | bytes 2097184 | tf_op jit(solution)/shard_map/ppermute | solution.py:85
  1212.6 4.5 subtract_reduce_fusion.41
  1252.7 4.4 collective-permute-start.20
  1262.7 45.7 %collective-permute-done.21 = f32[4,2,512,128]{3,2,1,0:T(8,128)S(1)} collective-permute-done((f32[4,2,512,128]{3,2,1,0:T(8,128)S(1)}, f32[4,2,512,128]{3,2,1,0:T(8,128)S(1)}, u32[]{:S(2)}, u32[]{:S(2)}) %collective-permute-start.21) | collective-permute-done | bytes 2097184 | tf_op jit(solution)/shard_map/ppermute | solution.py:85
  1312.0 44.6 %collective-permute-done.22 = f32[4,2,512,128]{3,2,1,0:T(8,128)S(1)} collective-permute-done((f32[4,2,512,128]{3,2,1,0:T(8,128)S(1)}, f32[4,2,512,128]{3,2,1,0:T(8,128)S(1)}, u32[]{:S(2)}, u32[]{:S(2)}) %collective-permute-start.22) | collective-permute-done | bytes 2097184 | tf_op jit(solution)/shard_map/ppermute | solution.py:85
  1357.7 44.6 %collective-permute-done.23 = f32[4,2,512,128]{3,2,1,0:T(8,128)S(1)} collective-permute-done((f32[4,2,512,128]{3,2,1,0:T(8,128)S(1)}, f32[4,2,512,128]{3,2,1,0:T(8,128)S(1)}, u32[]{:S(2)}, u32[]{:S(2)}) %collective-permute-start.23) | collective-permute-done | bytes 2097184 | tf_op jit(solution)/shard_map/ppermute | solution.py:85
  1405.1 43.6 %collective-permute-done.24 = f32[4,2,512,128]{3,2,1,0:T(8,128)S(1)} collective-permute-done((f32[4,2,512,128]{3,2,1,0:T(8,128)S(1)}, f32[4,2,512,128]{3,2,1,0:T(8,128)S(1)}, u32[]{:S(2)}, u32[]{:S(2)}) %collective-permute-start.24) | collective-permute-done | bytes 2097184 | tf_op jit(solution)/shard_map/ppermute | solution.py:85
  1489.8 4.4 collective-permute-start.25
  1500.4 45.7 %collective-permute-done.26 = f32[4,2,512,128]{3,2,1,0:T(8,128)S(1)} collective-permute-done((f32[4,2,512,128]{3,2,1,0:T(8,128)S(1)}, f32[4,2,512,128]{3,2,1,0:T(8,128)S(1)}, u32[]{:S(2)}, u32[]{:S(2)}) %collective-permute-start.26) | collective-permute-done | bytes 2097184 | tf_op jit(solution)/shard_map/ppermute | solution.py:85
  1550.2 44.6 %collective-permute-done.27 = f32[4,2,512,128]{3,2,1,0:T(8,128)S(1)} collective-permute-done((f32[4,2,512,128]{3,2,1,0:T(8,128)S(1)}, f32[4,2,512,128]{3,2,1,0:T(8,128)S(1)}, u32[]{:S(2)}, u32[]{:S(2)}) %collective-permute-start.27) | collective-permute-done | bytes 2097184 | tf_op jit(solution)/shard_map/ppermute | solution.py:85
  1596.4 44.6 %collective-permute-done.28 = f32[4,2,512,128]{3,2,1,0:T(8,128)S(1)} collective-permute-done((f32[4,2,512,128]{3,2,1,0:T(8,128)S(1)}, f32[4,2,512,128]{3,2,1,0:T(8,128)S(1)}, u32[]{:S(2)}, u32[]{:S(2)}) %collective-permute-start.28) | collective-permute-done | bytes 2097184 | tf_op jit(solution)/shard_map/ppermute | solution.py:85
  1650.7 39.3 %collective-permute-done.29 = f32[4,2,512,128]{3,2,1,0:T(8,128)} collective-permute-done((f32[4,2,512,128]{3,2,1,0:T(8,128)}, f32[4,2,512,128]{3,2,1,0:T(8,128)}, u32[]{:S(2)}, u32[]{:S(2)}) %collective-permute-start.29) | collective-permute-done | bytes 2097184 | tf_op jit(solution)/shard_map/ppermute | solution.py:85
  1693.8 48.5 %psum.7 = f32[2,7]{1,0:T(2,128)S(1)} all-reduce(f32[2,7]{1,0:T(2,128)S(1)} %concatenate.7211), channel_id=1, replica_groups=mesh['inst'=1,'qy'=4,'qx'=8] {'qy','qx'}, use_global_device_ids=true, to_apply=%region_67.68 | all-reduce | flops 14 | bytes 112 | tf_op jit(solution)/shard_map/psum | solution.py:95
  (1620 shorter events, 561.2 us)
Async XLA Ops:
  0.7 52.4 %copy-start.294 = (pred[128]{0:T(512)(128)(4,1)}, pred[128]{0:T(512)(128)(4,1)S(1)}, u32[]{:S(2)}) copy-start(pred[128]{0:T(512)(128)(4,1)S(1)} %get-tuple-element.2052) | copy-start | bytes 388
  0.7 62.2 %copy-start.291 = (pred[128]{0:T(512)(128)(4,1)}, pred[128]{0:T(512)(128)(4,1)S(1)}, u32[]{:S(2)}) copy-start(pred[128]{0:T(512)(128)(4,1)S(1)} %get-tuple-element.2055) | copy-start | bytes 388
  0.7 72.2 %copy-start.288 = (pred[128]{0:T(512)(128)(4,1)}, pred[128]{0:T(512)(128)(4,1)S(1)}, u32[]{:S(2)}) copy-start(pred[128]{0:T(512)(128)(4,1)S(1)} %get-tuple-element.2054) | copy-start | bytes 388
  0.7 82.1 %copy-start.285 = (pred[128]{0:T(512)(128)(4,1)}, pred[128]{0:T(512)(128)(4,1)S(1)}, u32[]{:S(2)}) copy-start(pred[128]{0:T(512)(128)(4,1)S(1)} %get-tuple-element.2057) | copy-start | bytes 388
  0.7 90.4 %copy-start.282 = (pred[128]{0:T(512)(128)(4,1)}, pred[128]{0:T(512)(128)(4,1)S(1)}, u32[]{:S(2)}) copy-start(pred[128]{0:T(512)(128)(4,1)S(1)} %get-tuple-element.2056) | copy-start | bytes 388
  0.7 102.7 %copy-start.255 = (pred[512]{0:T(512)(128)(4,1)}, pred[512]{0:T(512)(128)(4,1)S(1)}, u32[]{:S(2)}) copy-start(pred[512]{0:T(512)(128)(4,1)S(1)} %get-tuple-element.2059) | copy-start | bytes 1540
  0.7 111.0 %copy-start.271 = (pred[512]{0:T(512)(128)(4,1)}, pred[512]{0:T(512)(128)(4,1)S(1)}, u32[]{:S(2)}) copy-start(pred[512]{0:T(512)(128)(4,1)S(1)} %get-tuple-element.2058) | copy-start | bytes 1540
  0.8 120.6 %copy-start.268 = (pred[512]{0:T(512)(128)(4,1)}, pred[512]{0:T(512)(128)(4,1)S(1)}, u32[]{:S(2)}) copy-start(pred[512]{0:T(512)(128)(4,1)S(1)} %get-tuple-element.2061) | copy-start | bytes 1540
  0.8 130.4 %copy-start.252 = (pred[512]{0:T(512)(128)(4,1)}, pred[512]{0:T(512)(128)(4,1)S(1)}, u32[]{:S(2)}) copy-start(pred[512]{0:T(512)(128)(4,1)S(1)} %get-tuple-element.2060) | copy-start | bytes 1540
  0.8 140.2 %copy-start.249 = (pred[512]{0:T(512)(128)(4,1)}, pred[512]{0:T(512)(128)(4,1)S(1)}, u32[]{:S(2)}) copy-start(pred[512]{0:T(512)(128)(4,1)S(1)} %get-tuple-element.2063) | copy-start | bytes 1540
  0.8 149.8 %copy-start.265 = (pred[512]{0:T(512)(128)(4,1)}, pred[512]{0:T(512)(128)(4,1)S(1)}, u32[]{:S(2)}) copy-start(pred[512]{0:T(512)(128)(4,1)S(1)} %get-tuple-element.2062) | copy-start | bytes 1540
  0.8 159.2 %copy-start.258 = (pred[512]{0:T(512)(128)(4,1)}, pred[512]{0:T(512)(128)(4,1)S(1)}, u32[]{:S(2)}) copy-start(pred[512]{0:T(512)(128)(4,1)S(1)} %get-tuple-element.2064) | copy-start | bytes 1540
  0.8 159.2 %copy-start.262 = (pred[512]{0:T(512)(128)(4,1)}, pred[512]{0:T(512)(128)(4,1)S(1)}, u32[]{:S(2)}) copy-start(pred[512]{0:T(512)(128)(4,1)S(1)} %get-tuple-element.2065) | copy-start | bytes 1540
  18.2 528.3 %copy-start.217 = (f32[2]{0:T(128)}, f32[2]{0:T(128)S(1)}, u32[]{:S(2)}) copy-start(f32[2]{0:T(128)S(1)} %get-tuple-element.21) | copy-start | bytes 28
  18.2 528.3 %copy-start.219 = (f32[2]{0:T(128)}, f32[2]{0:T(128)S(1)}, u32[]{:S(2)}) copy-start(f32[2]{0:T(128)S(1)} %get-tuple-element.2044) | copy-start | bytes 28
  180.7 46.0 %copy-start.98 = (f32[1,2,512,126]{3,1,2,0:T(2,128)S(1)}, f32[1,2,512,126]{3,1,2,0:T(2,128)}, u32[]{:S(2)}) copy-start(f32[1,2,512,126]{3,1,2,0:T(2,128)} %get-tuple-element.1820) | copy-start | bytes 1548292
  180.7 46.0 %copy-start.99 = (f32[1,2,512,2]{3,1,2,0:T(2,128)S(1)}, f32[1,2,512,2]{3,1,2,0:T(2,128)}, u32[]{:S(2)}) copy-start(f32[1,2,512,2]{3,1,2,0:T(2,128)} %get-tuple-element.1815) | copy-start | bytes 24580
  180.8 46.0 %copy-start.100 = (f32[1,2,512,2]{3,1,2,0:T(2,128)S(1)}, f32[1,2,512,2]{3,1,2,0:T(2,128)}, u32[]{:S(2)}) copy-start(f32[1,2,512,2]{3,1,2,0:T(2,128)} %get-tuple-element.1816) | copy-start | bytes 24580
  180.8 46.0 %copy-start.115 = (f32[1,2,512,124]{3,1,2,0:T(2,128)S(1)}, f32[1,2,512,124]{3,1,2,0:T(2,128)}, u32[]{:S(2)}) copy-start(f32[1,2,512,124]{3,1,2,0:T(2,128)} %get-tuple-element.1827) | copy-start | bytes 1523716
  180.8 46.0 %copy-start.116 = (f32[1,2,512,124]{3,1,2,0:T(2,128)S(1)}, f32[1,2,512,124]{3,1,2,0:T(2,128)}, u32[]{:S(2)}) copy-start(f32[1,2,512,124]{3,1,2,0:T(2,128)} %get-tuple-element.1828) | copy-start | bytes 1523716
  180.8 46.0 %copy-start.117 = (f32[1,2,512,4]{3,1,2,0:T(2,128)S(1)}, f32[1,2,512,4]{3,1,2,0:T(2,128)}, u32[]{:S(2)}) copy-start(f32[1,2,512,4]{3,1,2,0:T(2,128)} %get-tuple-element.1823) | copy-start | bytes 49156
  180.8 46.0 %copy-start.118 = (f32[1,2,512,4]{3,1,2,0:T(2,128)S(1)}, f32[1,2,512,4]{3,1,2,0:T(2,128)}, u32[]{:S(2)}) copy-start(f32[1,2,512,4]{3,1,2,0:T(2,128)} %get-tuple-element.1824) | copy-start | bytes 49156
  180.8 46.0 %copy-start.121 = (f32[1,2,512,120]{3,1,2,0:T(2,128)S(1)}, f32[1,2,512,120]{3,1,2,0:T(2,128)}, u32[]{:S(2)}) copy-start(f32[1,2,512,120]{3,1,2,0:T(2,128)} %get-tuple-element.1835) | copy-start | bytes 1474564
  180.8 46.0 %copy-start.122 = (f32[1,2,512,120]{3,1,2,0:T(2,128)S(1)}, f32[1,2,512,120]{3,1,2,0:T(2,128)}, u32[]{:S(2)}) copy-start(f32[1,2,512,120]{3,1,2,0:T(2,128)} %get-tuple-element.1836) | copy-start | bytes 1474564
  180.8 46.0 %copy-start.123 = (f32[1,2,512,8]{3,1,2,0:T(2,128)S(1)}, f32[1,2,512,8]{3,1,2,0:T(2,128)}, u32[]{:S(2)}) copy-start(f32[1,2,512,8]{3,1,2,0:T(2,128)} %get-tuple-element.1831) | copy-start | bytes 98308
  180.8 46.0 %copy-start.124 = (f32[1,2,512,8]{3,1,2,0:T(2,128)S(1)}, f32[1,2,512,8]{3,1,2,0:T(2,128)}, u32[]{:S(2)}) copy-start(f32[1,2,512,8]{3,1,2,0:T(2,128)} %get-tuple-element.1832) | copy-start | bytes 98308
  180.8 46.0 %copy-start.144 = (f32[1,2,512,112]{3,1,2,0:T(2,128)S(1)}, f32[1,2,512,112]{3,1,2,0:T(2,128)}, u32[]{:S(2)}) copy-start(f32[1,2,512,112]{3,1,2,0:T(2,128)} %get-tuple-element.1843) | copy-start | bytes 1376260
  180.9 46.0 %copy-start.145 = (f32[1,2,512,112]{3,1,2,0:T(2,128)S(1)}, f32[1,2,512,112]{3,1,2,0:T(2,128)}, u32[]{:S(2)}) copy-start(f32[1,2,512,112]{3,1,2,0:T(2,128)} %get-tuple-element.1844) | copy-start | bytes 1376260
  180.9 46.0 %copy-start.150 = (f32[1,2,512,16]{3,1,2,0:T(2,128)S(1)}, f32[1,2,512,16]{3,1,2,0:T(2,128)}, u32[]{:S(2)}) copy-start(f32[1,2,512,16]{3,1,2,0:T(2,128)} %get-tuple-element.1839) | copy-start | bytes 196612
  180.9 46.0 %copy-start.151 = (f32[1,2,512,16]{3,1,2,0:T(2,128)S(1)}, f32[1,2,512,16]{3,1,2,0:T(2,128)}, u32[]{:S(2)}) copy-start(f32[1,2,512,16]{3,1,2,0:T(2,128)} %get-tuple-element.1840) | copy-start | bytes 196612
  180.9 46.0 %copy-start.156 = (f32[1,2,512,96]{3,1,2,0:T(2,128)S(1)}, f32[1,2,512,96]{3,1,2,0:T(2,128)}, u32[]{:S(2)}) copy-start(f32[1,2,512,96]{3,1,2,0:T(2,128)} %get-tuple-element.1851) | copy-start | bytes 1179652
  180.9 46.0 %copy-start.157 = (f32[1,2,512,96]{3,1,2,0:T(2,128)S(1)}, f32[1,2,512,96]{3,1,2,0:T(2,128)}, u32[]{:S(2)}) copy-start(f32[1,2,512,96]{3,1,2,0:T(2,128)} %get-tuple-element.1852) | copy-start | bytes 1179652
  180.9 46.0 %copy-start.160 = (f32[1,2,512,32]{3,1,2,0:T(2,128)S(1)}, f32[1,2,512,32]{3,1,2,0:T(2,128)}, u32[]{:S(2)}) copy-start(f32[1,2,512,32]{3,1,2,0:T(2,128)} %get-tuple-element.1847) | copy-start | bytes 393220
  180.9 46.0 %copy-start.161 = (f32[1,2,512,32]{3,1,2,0:T(2,128)S(1)}, f32[1,2,512,32]{3,1,2,0:T(2,128)}, u32[]{:S(2)}) copy-start(f32[1,2,512,32]{3,1,2,0:T(2,128)} %get-tuple-element.1848) | copy-start | bytes 393220
  268.7 4.4 collective-permute-start
  274.2 24.4 %collective-permute-start.1 = (f32[2,2,512,128]{3,1,2,0:T(2,128)S(1)}, f32[2,2,512,128]{3,1,2,0:T(2,128)S(1)}, u32[]{:S(2)}, u32[]{:S(2)}) collective-permute-start(f32[2,2,512,128]{3,1,2,0:T(2,128)S(1)} %pad_maximum_fusion.16), channel_id=1, source_target_pairs={{0,2},{1,3},{2,0},{3,1},{4,6},{5,7},{6,4},{7,5},{8,10},{9,11},{10,... | collective-permute-start | bytes 3145736 | tf_op jit(solution)/shard_map/ppermute | solution.py:70
  299.7 25.1 %collective-permute-start.2 = (f32[2,2,512,128]{3,1,2,0:T(2,128)S(1)}, f32[2,2,512,128]{3,1,2,0:T(2,128)S(1)}, u32[]{:S(2)}, u32[]{:S(2)}) collective-permute-start(f32[2,2,512,128]{3,1,2,0:T(2,128)S(1)} %pad_maximum_fusion.17), channel_id=1, source_target_pairs={{0,4},{1,5},{2,6},{3,7},{4,0},{5,1},{6,2},{7,3},{8,12},{9,13},{10,... | collective-permute-start | bytes 3145736 | tf_op jit(solution)/shard_map/ppermute | solution.py:70
  325.9 22.5 %collective-permute-start.3 = (f32[2,2,512,128]{3,1,2,0:T(2,128)S(1)}, f32[2,2,512,128]{3,1,2,0:T(2,128)S(1)}, u32[]{:S(2)}, u32[]{:S(2)}) collective-permute-start(f32[2,2,512,128]{3,1,2,0:T(2,128)S(1)} %pad_maximum_fusion.18), channel_id=1, source_target_pairs={{0,8},{8,0},{16,24},{24,16},{1,9},{9,1},{17,25},{25,17},{2,10},{10... | collective-permute-start | bytes 3145736 | tf_op jit(solution)/shard_map/ppermute | solution.py:70
  349.5 24.7 %collective-permute-start.4 = (f32[2,2,512,128]{3,1,2,0:T(2,128)S(1)}, f32[2,2,512,128]{3,1,2,0:T(2,128)S(1)}, u32[]{:S(2)}, u32[]{:S(2)}) collective-permute-start(f32[2,2,512,128]{3,1,2,0:T(2,128)S(1)} %pad_maximum_fusion.19), channel_id=1, source_target_pairs={{0,16},{8,24},{16,0},{24,8},{1,17},{9,25},{17,1},{25,9},{2,18},{10... | collective-permute-start | bytes 3145736 | tf_op jit(solution)/shard_map/ppermute | solution.py:70
  604.9 6.1 collective-permute-start.5
  612.9 24.4 %collective-permute-start.6 = (f32[2,2,512,128]{3,1,2,0:T(2,128)S(1)}, f32[2,2,512,128]{3,1,2,0:T(2,128)S(1)}, u32[]{:S(2)}, u32[]{:S(2)}) collective-permute-start(f32[2,2,512,128]{3,1,2,0:T(2,128)S(1)} %pad_maximum_fusion.21), channel_id=1, source_target_pairs={{0,2},{1,3},{2,0},{3,1},{4,6},{5,7},{6,4},{7,5},{8,10},{9,11},{10,... | collective-permute-start | bytes 3145736 | tf_op jit(solution)/shard_map/ppermute | solution.py:70
  639.3 25.1 %collective-permute-start.7 = (f32[2,2,512,128]{3,1,2,0:T(2,128)S(1)}, f32[2,2,512,128]{3,1,2,0:T(2,128)S(1)}, u32[]{:S(2)}, u32[]{:S(2)}) collective-permute-start(f32[2,2,512,128]{3,1,2,0:T(2,128)S(1)} %pad_maximum_fusion.22), channel_id=1, source_target_pairs={{0,4},{1,5},{2,6},{3,7},{4,0},{5,1},{6,2},{7,3},{8,12},{9,13},{10,... | collective-permute-start | bytes 3145736 | tf_op jit(solution)/shard_map/ppermute | solution.py:70
  665.1 22.5 %collective-permute-start.8 = (f32[2,2,512,128]{3,2,1,0:T(8,128)S(1)}, f32[2,2,512,128]{3,2,1,0:T(8,128)S(1)}, u32[]{:S(2)}, u32[]{:S(2)}) collective-permute-start(f32[2,2,512,128]{3,2,1,0:T(8,128)S(1)} %pad_maximum_fusion.23), channel_id=1, source_target_pairs={{0,8},{8,0},{16,24},{24,16},{1,9},{9,1},{17,25},{25,17},{2,10},{10... | collective-permute-start | bytes 3145736 | tf_op jit(solution)/shard_map/ppermute | solution.py:70
  689.1 23.1 %collective-permute-start.9 = (f32[2,2,512,128]{3,1,2,0:T(2,128)S(1)}, f32[2,2,512,128]{3,1,2,0:T(2,128)S(1)}, u32[]{:S(2)}, u32[]{:S(2)}) collective-permute-start(f32[2,2,512,128]{3,1,2,0:T(2,128)S(1)} %pad_maximum_fusion.24), channel_id=1, source_target_pairs={{0,16},{8,24},{16,0},{24,8},{1,17},{9,25},{17,1},{25,9},{2,18},{10... | collective-permute-start | bytes 3145736 | tf_op jit(solution)/shard_map/ppermute | solution.py:70
  863.5 6.7 collective-permute-start.10
  870.5 24.4 %collective-permute-start.11 = (f32[2,2,512,128]{3,2,1,0:T(8,128)S(1)}, f32[2,2,512,128]{3,2,1,0:T(8,128)S(1)}, u32[]{:S(2)}, u32[]{:S(2)}) collective-permute-start(f32[2,2,512,128]{3,2,1,0:T(8,128)S(1)} %pad_maximum_fusion.26), channel_id=1, source_target_pairs={{0,2},{1,3},{2,0},{3,1},{4,6},{5,7},{6,4},{7,5},{8,10},{9,11},{10,... | collective-permute-start | bytes 3145736 | tf_op jit(solution)/shard_map/ppermute | solution.py:70
  895.3 25.1 %collective-permute-start.12 = (f32[2,2,512,128]{3,2,1,0:T(8,128)S(1)}, f32[2,2,512,128]{3,2,1,0:T(8,128)S(1)}, u32[]{:S(2)}, u32[]{:S(2)}) collective-permute-start(f32[2,2,512,128]{3,2,1,0:T(8,128)S(1)} %pad_maximum_fusion.27), channel_id=1, source_target_pairs={{0,4},{1,5},{2,6},{3,7},{4,0},{5,1},{6,2},{7,3},{8,12},{9,13},{10,... | collective-permute-start | bytes 3145736 | tf_op jit(solution)/shard_map/ppermute | solution.py:70
  921.0 22.5 %collective-permute-start.13 = (f32[2,2,512,128]{3,2,1,0:T(8,128)S(1)}, f32[2,2,512,128]{3,2,1,0:T(8,128)S(1)}, u32[]{:S(2)}, u32[]{:S(2)}) collective-permute-start(f32[2,2,512,128]{3,2,1,0:T(8,128)S(1)} %pad_maximum_fusion.28), channel_id=1, source_target_pairs={{0,8},{8,0},{16,24},{24,16},{1,9},{9,1},{17,25},{25,17},{2,10},{10... | collective-permute-start | bytes 3145736 | tf_op jit(solution)/shard_map/ppermute | solution.py:70
  943.8 24.9 %collective-permute-start.14 = (f32[2,2,512,128]{3,2,1,0:T(8,128)S(1)}, f32[2,2,512,128]{3,2,1,0:T(8,128)S(1)}, u32[]{:S(2)}, u32[]{:S(2)}) collective-permute-start(f32[2,2,512,128]{3,2,1,0:T(8,128)S(1)} %pad_maximum_fusion.29), channel_id=1, source_target_pairs={{0,16},{8,24},{16,0},{24,8},{1,17},{9,25},{17,1},{25,9},{2,18},{10... | collective-permute-start | bytes 3145736 | tf_op jit(solution)/shard_map/ppermute | solution.py:70
  1010.4 7.3 collective-permute-start.15
  1018.9 46.9 %collective-permute-start.16 = (f32[4,2,512,128]{3,2,1,0:T(8,128)S(1)}, f32[4,2,512,128]{3,2,1,0:T(8,128)S(1)}, u32[]{:S(2)}, u32[]{:S(2)}) collective-permute-start(f32[4,2,512,128]{3,2,1,0:T(8,128)S(1)} %pad_maximum_fusion.1), channel_id=1, source_target_pairs={{0,2},{1,3},{2,0},{3,1},{4,6},{5,7},{6,4},{7,5},{8,10},{9,11},{10,... | collective-permute-start | bytes 6291464 | tf_op jit(solution)/shard_map/ppermute | solution.py:85
  1067.1 47.6 %collective-permute-start.17 = (f32[4,2,512,128]{3,2,1,0:T(8,128)S(1)}, f32[4,2,512,128]{3,2,1,0:T(8,128)S(1)}, u32[]{:S(2)}, u32[]{:S(2)}) collective-permute-start(f32[4,2,512,128]{3,2,1,0:T(8,128)S(1)} %pad_maximum_fusion.2), channel_id=1, source_target_pairs={{0,4},{1,5},{2,6},{3,7},{4,0},{5,1},{6,2},{7,3},{8,12},{9,13},{10,... | collective-permute-start | bytes 6291464 | tf_op jit(solution)/shard_map/ppermute | solution.py:85
  1115.8 45.0 %collective-permute-start.18 = (f32[4,2,512,128]{3,2,1,0:T(8,128)S(1)}, f32[4,2,512,128]{3,2,1,0:T(8,128)S(1)}, u32[]{:S(2)}, u32[]{:S(2)}) collective-permute-start(f32[4,2,512,128]{3,2,1,0:T(8,128)S(1)} %pad_maximum_fusion.3), channel_id=1, source_target_pairs={{0,8},{8,0},{16,24},{24,16},{1,9},{9,1},{17,25},{25,17},{2,10},{10... | collective-permute-start | bytes 6291464 | tf_op jit(solution)/shard_map/ppermute | solution.py:85
  1161.9 45.6 %collective-permute-start.19 = (f32[4,2,512,128]{3,2,1,0:T(8,128)S(1)}, f32[4,2,512,128]{3,2,1,0:T(8,128)S(1)}, u32[]{:S(2)}, u32[]{:S(2)}) collective-permute-start(f32[4,2,512,128]{3,2,1,0:T(8,128)S(1)} %pad_maximum_fusion.4), channel_id=1, source_target_pairs={{0,16},{8,24},{16,0},{24,8},{1,17},{9,25},{17,1},{25,9},{2,18},{10... | collective-permute-start | bytes 6291464 | tf_op jit(solution)/shard_map/ppermute | solution.py:85
  1252.7 8.2 collective-permute-start.20
  1261.5 46.9 %collective-permute-start.21 = (f32[4,2,512,128]{3,2,1,0:T(8,128)S(1)}, f32[4,2,512,128]{3,2,1,0:T(8,128)S(1)}, u32[]{:S(2)}, u32[]{:S(2)}) collective-permute-start(f32[4,2,512,128]{3,2,1,0:T(8,128)S(1)} %pad_maximum_fusion.6), channel_id=1, source_target_pairs={{0,2},{1,3},{2,0},{3,1},{4,6},{5,7},{6,4},{7,5},{8,10},{9,11},{10,... | collective-permute-start | bytes 6291464 | tf_op jit(solution)/shard_map/ppermute | solution.py:85
  1309.1 47.6 %collective-permute-start.22 = (f32[4,2,512,128]{3,2,1,0:T(8,128)S(1)}, f32[4,2,512,128]{3,2,1,0:T(8,128)S(1)}, u32[]{:S(2)}, u32[]{:S(2)}) collective-permute-start(f32[4,2,512,128]{3,2,1,0:T(8,128)S(1)} %pad_maximum_fusion.7), channel_id=1, source_target_pairs={{0,4},{1,5},{2,6},{3,7},{4,0},{5,1},{6,2},{7,3},{8,12},{9,13},{10,... | collective-permute-start | bytes 6291464 | tf_op jit(solution)/shard_map/ppermute | solution.py:85
  1357.3 45.0 %collective-permute-start.23 = (f32[4,2,512,128]{3,2,1,0:T(8,128)S(1)}, f32[4,2,512,128]{3,2,1,0:T(8,128)S(1)}, u32[]{:S(2)}, u32[]{:S(2)}) collective-permute-start(f32[4,2,512,128]{3,2,1,0:T(8,128)S(1)} %pad_maximum_fusion.8), channel_id=1, source_target_pairs={{0,8},{8,0},{16,24},{24,16},{1,9},{9,1},{17,25},{25,17},{2,10},{10... | collective-permute-start | bytes 6291464 | tf_op jit(solution)/shard_map/ppermute | solution.py:85
  1403.0 45.6 %collective-permute-start.24 = (f32[4,2,512,128]{3,2,1,0:T(8,128)S(1)}, f32[4,2,512,128]{3,2,1,0:T(8,128)S(1)}, u32[]{:S(2)}, u32[]{:S(2)}) collective-permute-start(f32[4,2,512,128]{3,2,1,0:T(8,128)S(1)} %pad_maximum_fusion.9), channel_id=1, source_target_pairs={{0,16},{8,24},{16,0},{24,8},{1,17},{9,25},{17,1},{25,9},{2,18},{10... | collective-permute-start | bytes 6291464 | tf_op jit(solution)/shard_map/ppermute | solution.py:85
  1489.8 8.2 collective-permute-start.25
  1499.1 46.9 %collective-permute-start.26 = (f32[4,2,512,128]{3,2,1,0:T(8,128)S(1)}, f32[4,2,512,128]{3,2,1,0:T(8,128)S(1)}, u32[]{:S(2)}, u32[]{:S(2)}) collective-permute-start(f32[4,2,512,128]{3,2,1,0:T(8,128)S(1)} %pad_maximum_fusion.11), channel_id=1, source_target_pairs={{0,2},{1,3},{2,0},{3,1},{4,6},{5,7},{6,4},{7,5},{8,10},{9,11},{10,... | collective-permute-start | bytes 6291464 | tf_op jit(solution)/shard_map/ppermute | solution.py:85
  1547.3 47.6 %collective-permute-start.27 = (f32[4,2,512,128]{3,2,1,0:T(8,128)S(1)}, f32[4,2,512,128]{3,2,1,0:T(8,128)S(1)}, u32[]{:S(2)}, u32[]{:S(2)}) collective-permute-start(f32[4,2,512,128]{3,2,1,0:T(8,128)S(1)} %pad_maximum_fusion.12), channel_id=1, source_target_pairs={{0,4},{1,5},{2,6},{3,7},{4,0},{5,1},{6,2},{7,3},{8,12},{9,13},{10,... | collective-permute-start | bytes 6291464 | tf_op jit(solution)/shard_map/ppermute | solution.py:85
  1596.0 45.0 %collective-permute-start.28 = (f32[4,2,512,128]{3,2,1,0:T(8,128)S(1)}, f32[4,2,512,128]{3,2,1,0:T(8,128)S(1)}, u32[]{:S(2)}, u32[]{:S(2)}) collective-permute-start(f32[4,2,512,128]{3,2,1,0:T(8,128)S(1)} %pad_maximum_fusion.13), channel_id=1, source_target_pairs={{0,8},{8,0},{16,24},{24,16},{1,9},{9,1},{17,25},{25,17},{2,10},{10... | collective-permute-start | bytes 6291464 | tf_op jit(solution)/shard_map/ppermute | solution.py:85
  1644.2 45.7 %collective-permute-start.29 = (f32[4,2,512,128]{3,2,1,0:T(8,128)}, f32[4,2,512,128]{3,2,1,0:T(8,128)}, u32[]{:S(2)}, u32[]{:S(2)}) collective-permute-start(f32[4,2,512,128]{3,2,1,0:T(8,128)} %pad_maximum_fusion.14), channel_id=1, source_target_pairs={{0,16},{8,24},{16,0},{24,8},{1,17},{9,25},{17,1},{25,9},{2,18},{10... | collective-permute-start | bytes 6291464 | tf_op jit(solution)/shard_map/ppermute | solution.py:85
  (337 other events, 3051.4 us)
where the time goes:
time: 1750 us; the launch traced here: 1740 us
  waiting for transfers between devices  809 us (46%)
  other arithmetic  502 us (29%)
  local copies, waits for them, and re-layouts  308 us (18%)
  starting transfers between devices  66.7 us (4%)
  blocking collectives  48.5 us (3%)
    ppermute x15, waiting for transfers between devices, device_fn(): partner = lax.ppermute(jnp.stack(list(four_amps)), axis_name, pair_list)  543 us
    ppermute x15, waiting for transfers between devices, device_fn(): partner = lax.ppermute(jnp.stack([psi_re, psi_im]), axis_name, pair_list)  267 us
    concatenate x129, local copies, waits for them, and re-layouts, flip_grid(): jnp.roll(amplitudes, shift, axis=axis_pos)  154 us
    add x27, other arithmetic, device_fn(): cos_b * psi_re + sin_b * flip_im  124 us
    sub x26, other arithmetic, device_fn(): cos_b * psi_im - sin_b * flip_re  107 us
    reduce_sum x61, other arithmetic, inverse_step(): term = jnp.sum(lam_re * partner[1] - lam_im * partner[0], axis=(1, 2))  78 us
    concatenate x58, local copies, waits for them, and re-layouts, flip_grid(): jnp.roll(amplitudes, -shift, axis=axis_pos)  74 us
    slice x387, local copies, waits for them, and re-layouts, flip_grid(): jnp.roll(amplitudes, shift, axis=axis_pos)  51.8 us
  transfers between devices with their start and end apart: 30, of which 30 were waited for; matrix products, arithmetic and copies ran while one was open for 0% of the time, Pallas kernels for 0%

commit v1 on v0

v1 whole, which is shorter than its diff:
```python
import functools
import jax
import jax.numpy as jnp
from jax import lax
from jax.experimental import pallas as pl
from jax.experimental.pallas import tpu as pltpu
from jax.sharding import PartitionSpec as P

LANE = 128
LANE_BITS = 7
SUB = 8
MESH_ID = pl.DeviceIdType.MESH
F32 = jnp.float32
BF16 = jnp.bfloat16


def sincos(x):
    k = jnp.floor(x * 0.6366197723675814 + 0.5)
    r = ((x - k * 1.5703125) - k * 4.837512969970703125e-4) - k * 7.54978995489188216e-8
    z = r * r
    s = r + r * z * (-1.6666654611e-1 + z * (8.3321608736e-3 + z * -1.9515295891e-4))
    c = (1.0 - 0.5 * z) + z * z * (4.166664568298827e-2 + z * (-1.388731625493765e-3 + z * 2.443315711809948e-5))
    q = k.astype(jnp.int32)
    odd = (q & 1) != 0
    sin_v = jnp.where(odd, c, s)
    cos_v = jnp.where(odd, s, c)
    sin_v = jnp.where((q & 2) != 0, -sin_v, sin_v)
    cos_v = jnp.where(((q + 1) & 2) != 0, -cos_v, cos_v)
    return sin_v, cos_v


def split3(x):
    hi = x.astype(BF16)
    rest = x - hi.astype(F32)
    mid = rest.astype(BF16)
    low = (rest - mid.astype(F32)).astype(BF16)
    return hi, mid, low


def mm(a, b):
    return jnp.dot(a, b, preferred_element_type=F32)


def rot(pairs, stride, c, t):
    out = list(pairs)
    for j in range(len(pairs)):
        if j & stride:
            continue
        (ar, ai), (br, bi) = pairs[j], pairs[j | stride]
        out[j] = (c * ar + t * bi, c * ai - t * br)
        out[j | stride] = (c * br + t * ai, c * bi - t * ar)
    return out


def sub_flip(x, bit):
    if bit == 2:
        return pltpu.roll(x, 4, 0)
    row = lax.broadcasted_iota(jnp.int32, (SUB, LANE), 0)
    up = pltpu.roll(x, 1 << bit, 0)
    down = pltpu.roll(x, SUB - (1 << bit), 0)
    return jnp.where((row & (1 << bit)) != 0, up, down)


def make_kernel(ny, nx, num_sets, num_layers, rows, norm):
    n = ny * nx
    lo = 8
    hi = n // lo
    tiles = rows // SUB
    lo_bits = [1 << b for b in range(lo.bit_length() - 1)]
    hi_bits = [1 << b for b in range(hi.bit_length() - 1)]
    tile_bits = [1 << b for b in range(tiles.bit_length() - 1)]
    width_x = nx // 2

    def order(a):
        return 2 - a + (a // 2) * (7 - 2 * a)

    def kernel(cost_ref, gamma_ref, beta_ref, e_ref, g_ref,
               cost_b, src, dst, keep, tab, psi_b, psi_c, wmat, adj, dmat, ct, acc, mine, parts, tmp, send_sem, recv_sem):
        qy = lax.axis_index('qy')
        qx = lax.axis_index('qx')
        me = qy * nx + qx
        barrier = pltpu.get_barrier_semaphore()

        def each_peer(act):
            def body(i, _):
                ty = lax.rem(qy + order(i // (2 * width_x)), ny)
                tx = lax.rem(qx // 2 + order(lax.rem(i // 2, width_x)), width_x) * 2 + lax.rem(qx + 1 + i, 2)
                act(ty, tx)
                return 0
            lax.fori_loop(0, n - 1, body, 0)

        def greet(ty, tx):
            pl.semaphore_signal(barrier, inc=1, device_id={'qy': ty, 'qx': tx}, device_id_type=MESH_ID)
        each_peer(greet)

        def send(source, target, ids, ty, tx):
            pltpu.make_async_remote_copy(
                source, target, send_sem.at[ids], recv_sem.at[ids],
                device_id={'qy': ty, 'qx': tx}, device_id_type=MESH_ID).start()

        def exchange(source, target, ids):
            each_peer(lambda ty, tx: send(source.at[ty * nx + tx], target.at[me], ids, ty, tx))

        def wait_bytes(buf, sem):
            part = buf.at[pl.ds(0, n - 1)]
            pltpu.make_async_copy(part, part, sem).wait()

        def tile_d(r, _):
            a = lax.broadcasted_iota(jnp.int32, (SUB, LANE), 0) + r * SUB
            b = lax.broadcasted_iota(jnp.int32, (SUB, LANE), 1)
            x = a ^ b
            d = jnp.zeros_like(x)
            for k in range(LANE_BITS):
                d = d + ((x >> k) & 1)
            dmat[pl.ds(pl.multiple_of(r * SUB, SUB), SUB), :] = d
            return 0
        lax.fori_loop(0, LANE // SUB, tile_d, 0)
        one = (dmat[...] == 1).astype(F32).astype(BF16)
        zero = jnp.zeros((LANE, LANE), BF16)
        adj[0:LANE, 0:LANE] = one
        adj[0:LANE, LANE:] = zero
        adj[LANE:, 0:LANE] = zero
        adj[LANE:, LANE:] = one
        for s in range(num_sets):
            for l in range(num_layers):
                k = s * num_layers + l
                sin_h, cos_h = sincos(jnp.full((SUB, LANE), 0.5 * beta_ref[s, l], F32))
                ct[k, 0] = cos_h
                ct[k, 1] = sin_h
                ct[k, 2] = -sin_h

        def weights(k, slot):
            c, t = ct[k, 0], ct[k, 1]
            cp, tp = [jnp.ones_like(c)], [jnp.ones_like(c)]
            for _ in range(LANE_BITS):
                cp.append(cp[-1] * c)
                tp.append(tp[-1] * t)
            amp = [cp[LANE_BITS - d] * tp[d] for d in range(LANE_BITS + 1)]
            z = jnp.zeros_like(c)
            real = [z, z, z, z, z, z, z, z]
            imag = [z, z, z, z, z, z, z, z]
            for d in range(LANE_BITS + 1):
                if d % 4 == 0:
                    real[d] = amp[d]
                elif d % 4 == 1:
                    imag[d] = -amp[d]
                elif d % 4 == 2:
                    real[d] = -amp[d]
                else:
                    imag[d] = amp[d]

            def body(r, _):
                at = pl.multiple_of(r * 2 * SUB, 2 * SUB)
                rows_re, rows_im = [], []
                for h in range(2):
                    d = dmat[pl.ds(at + h * SUB, SUB), :]
                    re = z
                    im = z
                    for j in range(LANE_BITS + 1):
                        hit = d == j
                        if j % 2 == 0:
                            re = jnp.where(hit, real[j], re)
                        else:
                            im = jnp.where(hit, imag[j], im)
                    rows_re.append(re)
                    rows_im.append(im)
                re = jnp.concatenate(rows_re, axis=0)
                im = jnp.concatenate(rows_im, axis=0)
                for p, (a, b) in enumerate(zip(split3(re), split3(im))):
                    top = pl.ds(at, 2 * SUB)
                    bot = pl.ds(at + LANE, 2 * SUB)
                    wmat[slot, 0, p, top, 0:LANE] = a
                    wmat[slot, 0, p, top, LANE:] = b
                    wmat[slot, 0, p, bot, 0:LANE] = -b
                    wmat[slot, 0, p, bot, LANE:] = a
                    wmat[slot, 1, p, top, 0:LANE] = a
                    wmat[slot, 1, p, top, LANE:] = -b
                    wmat[slot, 1, p, bot, 0:LANE] = b
                    wmat[slot, 1, p, bot, LANE:] = a
                return 0
            lax.fori_loop(0, LANE // (2 * SUB), body, 0)

        def tile_rows(tile):
            return pl.ds(pl.multiple_of(tile * SUB, SUB), SUB)

        def load(ref, slot, tile):
            r = tile_rows(tile)
            return ref[slot, r, 0:LANE], ref[slot, r, LANE:]

        def store(ref, slot, tile, pair):
            r = tile_rows(tile)
            ref[slot, r, 0:LANE] = pair[0]
            ref[slot, r, LANE:] = pair[1]

        def mix_low(source, target, k, sign):
            c, t = ct[k, 0], ct[k, sign]

            def body(i, _):
                base, tile = (i // tiles) * lo, i % tiles
                v = [load(source, base + j, tile) for j in range(lo)]
                for b in lo_bits:
                    v = rot(v, b, c, t)
                for j in range(lo):
                    store(target, base + j, tile, v[j])
                return 0
            lax.fori_loop(0, hi * tiles, body, 0)

        def mid_pass(source, target, k_in, s_in, k_out, s_out, middle):
            if k_in is not None:
                c0, t0 = ct[k_in, 0], ct[k_in, s_in]
            if k_out is not None:
                c1, t1 = ct[k_out, 0], ct[k_out, s_out]

            def body(i, carry):
                base, tile = i // tiles, i % tiles
                slots = [base + j * lo for j in range(hi)]
                if source is None:
                    v = [None] * hi
                else:
                    v = [load(source, m, tile) for m in slots]
                if k_in is not None:
                    for b in hi_bits:
                        v = rot(v, b, c0, t0)
                v, carry = middle(v, slots, tile, carry)
                if k_out is not None:
                    for b in hi_bits:
                        v = rot(v, b, c1, t1)
                    for j in range(hi):
                        store(target, slots[j], tile, v[j])
                return carry
            return lax.fori_loop(0, lo * tiles, body, jnp.zeros((SUB, LANE), F32))

        def pre_mix(source, target, k, sign):
            c, t = ct[k, 0], ct[k, sign]

            def rows_body(i, _):
                base = i * lo
                v = [load(source, base + j // tiles, j % tiles) for j in range(lo * tiles)]
                for b in lo_bits:
                    v = rot(v, b * tiles, c, t)
                for b in tile_bits:
                    v = rot(v, b, c, t)
                for j in range(lo * tiles):
                    re, im = v[j]
                    for b in range(3):
                        fr, fi = sub_flip(re, b), sub_flip(im, b)
                        re, im = c * re + t * fi, c * im - t * fr
                    store(tmp, base + j // tiles, j % tiles, (re, im))
                return 0
            lax.fori_loop(0, hi, rows_body, 0)

            def lanes_body(i, _):
                at = pl.ds(pl.multiple_of(i * lo, lo), lo)
                x = tmp[at].reshape(lo * rows, 2 * LANE)
                xh, xm, xl = split3(x)
                w = [wmat[k, sign - 1, p] for p in range(3)]
                y = mm(xh, w[0]) + (mm(xh, w[1]) + mm(xm, w[0])) + (mm(xh, w[2]) + mm(xm, w[1]) + mm(xl, w[0]))
                target[at] = y.reshape(lo, rows, 2 * LANE)
                return 0
            lax.fori_loop(0, hi, lanes_body, 0)

        def im_dot(a, b):
            return a[0] * b[1] - a[1] * b[0]

        def slot_dot(bra, ket):
            def group(slots, tile, bits, a):
                x = [load(bra, m, tile) for m in slots]
                y = [load(ket, m, tile) for m in slots]
                for j in range(len(slots)):
                    re = sum(y[j ^ b][0] for b in bits[1:]) + y[j ^ bits[0]][0] if len(bits) > 1 else y[j ^ bits[0]][0]
                    im = sum(y[j ^ b][1] for b in bits[1:]) + y[j ^ bits[0]][1] if len(bits) > 1 else y[j ^ bits[0]][1]
                    a = a + im_dot(x[j], (re, im))
                return a

            def low(i, a):
                return group([(i // tiles) * lo + j for j in range(lo)], i % tiles, lo_bits, a)

            def high(i, a):
                return group([i // tiles + j * lo for j in range(hi)], i % tiles, hi_bits, a)
            a = lax.fori_loop(0, hi * tiles, low, jnp.zeros((SUB, LANE), F32))
            return lax.fori_loop(0, lo * tiles, high, a)

        def fold(x):
            while x.shape[0] > SUB:
                half = x.shape[0] // 2
                x = x[:half] + x[half:]
            return x

        def inner_x(x):
            xh, xm, xl = split3(x)
            y = mm(xh, adj[...]) + mm(xm, adj[...]) + mm(xl, adj[...])
            return y

        def tile_flips(v):
            out = []
            for j in range(len(v)):
                parts_ = []
                for comp in range(2):
                    x = v[j][comp]
                    f = sub_flip(x, 0) + sub_flip(x, 1) + sub_flip(x, 2)
                    for b in tile_bits:
                        f = f + v[j ^ b][comp]
                    parts_.append(f)
                out.append(tuple(parts_))
            return out

        def inner_apply(ket, target):
            def body(i, _):
                at = pl.ds(pl.multiple_of(i * lo, lo), lo)
                y = inner_x(ket[at].reshape(lo * rows, 2 * LANE))
                target[at] = y.reshape(lo, rows, 2 * LANE)
                return 0
            lax.fori_loop(0, hi, body, 0)

            def add(i, _):
                v = [load(ket, i, j) for j in range(tiles)]
                f = tile_flips(v)
                for j in range(tiles):
                    y = load(target, i, j)
                    store(target, i, j, (y[0] + f[j][0], y[1] + f[j][1]))
                return 0
            lax.fori_loop(0, n, add, 0)

        def inner_dots(bra, ket, cost):
            inner_apply(ket, tmp)

            def body(i, carry):
                a, g = carry
                for j in range(tiles):
                    x = load(bra, i, j)
                    a = a + im_dot(x, load(tmp, i, j))
                    g = g + cost[i, tile_rows(j), :] * im_dot(x, load(ket, i, j))
                return a, g
            z = jnp.zeros((SUB, LANE), F32)
            return lax.fori_loop(0, n, body, (z, z))

        def two_dots(bra, ket_b, ket_c):
            def body(i, carry):
                a, g = carry
                for j in range(tiles):
                    x = load(bra, i, j)
                    a = a + im_dot(x, load(ket_b, i, j))
                    g = g + im_dot(x, load(ket_c, i, j))
                return a, g
            z = jnp.zeros((SUB, LANE), F32)
            return lax.fori_loop(0, n, body, (z, z))

        def slot_x(source, target):
            def low(i, _):
                base, tile = (i // tiles) * lo, i % tiles
                y = [load(source, base + j, tile) for j in range(lo)]
                for j in range(lo):
                    o = load(target, base + j, tile)
                    store(target, base + j, tile, tuple(o[c] + (y[j ^ 1][c] + y[j ^ 2][c] + y[j ^ 4][c]) for c in range(2)))
                return 0
            lax.fori_loop(0, hi * tiles, low, 0)

            def high(i, _):
                base, tile = i // tiles, i % tiles
                y = [load(source, base + j * lo, tile) for j in range(hi)]
                for j in range(hi):
                    o = load(target, base + j * lo, tile)
                    store(target, base + j * lo, tile, tuple(o[c] + (y[j ^ 1][c] + y[j ^ 2][c]) for c in range(2)))
                return 0
            lax.fori_loop(0, lo * tiles, high, 0)

        def slot_mix_all(ref, k):
            mix_low(ref, ref, k, 1)
            mid_pass(ref, ref, None, 1, k, 1, lambda v, slots, tile, a: (v, a))

        def fill_table(ref, cost, s, l, scale):
            g = gamma_ref[s, l]

            def body(i, _):
                for j in range(tiles):
                    sn, cs = sincos(cost[i, tile_rows(j), :] * g)
                    if scale is None:
                        store(ref, i, j, (cs, sn))
                    else:
                        store(ref, i, j, (cs * scale, sn * -scale))
                return 0
            lax.fori_loop(0, n, body, 0)

        def own(source, target):
            target[me] = source[me]

        def stage(e, s, e_next, k_in, s_in, k_out, s_out, middle):
            wait_bytes(dst.at[e, s], recv_sem.at[e, s])
            mix_low(dst.at[e, s], tmp, k_in, s_in)
            a = mid_pass(tmp, tmp, k_in, s_in, k_out, s_out, middle)
            pre_mix(tmp, src.at[e_next, s], k_out, s_out)
            own(src.at[e_next, s], dst.at[e_next, s])
            exchange(src.at[e_next, s], dst.at[e_next, s], (e_next, s))
            return a

        def kk(s, l):
            return s * num_layers + l

        def add_acc(s, q, a, init=False):
            row = s * 8 + q
            acc[row] = a if init else acc[row] + a


        def set_weights(k, _):
            weights(k, k)
            return 0
        lax.fori_loop(0, num_sets * num_layers, set_weights, 0)
        pl.semaphore_wait(barrier, n - 1)
        exchange(cost_ref, cost_b, (6, 0))

        def each_set(f):
            lax.fori_loop(0, num_sets, lambda s, _: (f(s), 0)[1], 0)

        cost_b[me] = cost_ref[me]

        @each_set
        def _(s):
            fill_table(keep.at[0, s], cost_ref, s, 0, norm)
            mid_pass(keep.at[0, s], tmp, None, 1, kk(s, 0), 1, lambda v, slots, tile, a: (v, a))
            pre_mix(tmp, src.at[0, s], kk(s, 0), 1)
            own(src.at[0, s], dst.at[0, s])
            exchange(src.at[0, s], dst.at[0, s], (0, s))

        wait_bytes(cost_b, recv_sem.at[6, 0])
        @each_set
        def _(s):
            fill_table(tab.at[0, s], cost_b, s, 1, None)
        @each_set
        def _(s):
            fill_table(tab.at[1, s], cost_ref, s, 2, None)

        def forward_mid(before, after, table):
            def middle(v, slots, tile, a):
                out = []
                for m, (re, im) in zip(slots, v):
                    store(before, m, tile, (re, im))
                    cs, sn = load(table, m, tile)
                    p = (re * cs + im * sn, im * cs - re * sn)
                    store(after, m, tile, p)
                    out.append(p)
                return out, a
            return middle

        def backward_mid(before, after, table):
            def middle(v, slots, tile, a):
                out = []
                for m, (re, im) in zip(slots, v):
                    store(before, m, tile, (re, im))
                    cs, sn = load(table, m, tile)
                    p = (re * cs - im * sn, im * cs + re * sn)
                    store(after, m, tile, p)
                    out.append(p)
                return out, a
            return middle

        def turn_mid(psi, lam):
            def middle(v, slots, tile, a):
                out = []
                for m, (re, im) in zip(slots, v):
                    store(psi, m, tile, (re, im))
                    w = cost_b[m, tile_rows(tile), :]
                    p = (w * re, w * im)
                    a = a + (p[0] * re + p[1] * im)
                    store(lam, m, tile, p)
                    out.append(p)
                return out, a
            return middle

        @each_set
        def _(s):
            stage(0, s, 1, kk(s, 0), 1, kk(s, 1), 1, forward_mid(keep.at[1, s], keep.at[2, s], tab.at[0, s]))
        @each_set
        def _(s):
            stage(1, s, 2, kk(s, 1), 1, kk(s, 2), 1, forward_mid(keep.at[3, s], keep.at[4, s], tab.at[1, s]))
            inner_apply(keep.at[0, s], psi_b.at[s])
            slot_x(keep.at[0, s], psi_b.at[s])
            slot_mix_all(psi_b.at[s], kk(s, 0))

            def times_cost(i, _):
                for j in range(tiles):
                    re, im = load(keep.at[0, s], i, j)
                    w = cost_ref[i, tile_rows(j), :]
                    store(psi_c.at[s], i, j, (w * re, w * im))
                return 0
            lax.fori_loop(0, n, times_cost, 0)
            slot_mix_all(psi_c.at[s], kk(s, 0))
        @each_set
        def _(s):
            a = stage(2, s, 3, kk(s, 2), 1, kk(s, 2), 2, turn_mid(keep.at[5, s], keep.at[6, s]))
            add_acc(s, 0, a, True)
            add_acc(s, 6, slot_dot(keep.at[6, s], keep.at[5, s]), True)
        @each_set
        def _(s):
            stage(3, s, 4, kk(s, 2), 2, kk(s, 1), 2, backward_mid(keep.at[7, s], keep.at[8, s], tab.at[1, s]))
            b, g = inner_dots(keep.at[7, s], keep.at[4, s], cost_ref)
            add_acc(s, 6, b + slot_dot(keep.at[7, s], keep.at[4, s]))
            add_acc(s, 3, 2.0 * g, True)
            add_acc(s, 5, slot_dot(keep.at[8, s], keep.at[3, s]), True)
        @each_set
        def _(s):
            stage(4, s, 5, kk(s, 1), 2, kk(s, 0), 2, backward_mid(keep.at[9, s], keep.at[10, s], tab.at[0, s]))
            b, g = inner_dots(keep.at[9, s], keep.at[2, s], cost_b)
            add_acc(s, 5, b + slot_dot(keep.at[9, s], keep.at[2, s]))
            add_acc(s, 2, 2.0 * g, True)
            add_acc(s, 4, slot_dot(keep.at[10, s], keep.at[1, s]), True)
        @each_set
        def _(s):
            wait_bytes(dst.at[5, s], recv_sem.at[5, s])
            b, g = two_dots(dst.at[5, s], psi_b.at[s], psi_c.at[s])
            add_acc(s, 4, b)
            add_acc(s, 1, 2.0 * g, True)

        lane = lax.broadcasted_iota(jnp.int32, (1, LANE), 1)
        vec = jnp.zeros((1, LANE), F32)
        for s in range(num_sets):
            for q in range(1 + 2 * num_layers):
                total = jnp.sum(jnp.sum(acc[s * 8 + q], axis=0, keepdims=True), axis=1, keepdims=True)
                vec = jnp.where(lane == s * 8 + q, total, vec)
        mine[0] = jnp.broadcast_to(vec, (SUB, LANE))
        parts[me] = jnp.broadcast_to(vec, (SUB, LANE))
        each_peer(lambda ty, tx: send(mine.at[0], parts.at[me], (6, 1), ty, tx))
        wait_bytes(parts, recv_sem.at[6, 1])
        total = parts[0]
        for m in range(1, n):
            total = total + parts[m]
        for s in range(num_sets):
            e_ref[s] = total[0, s * 8]
            for q in range(2 * num_layers):
                g_ref[s, q] = total[0, s * 8 + 1 + q]

        for e in range(6):
            for s in range(num_sets):
                wait_bytes(src.at[e, s], send_sem.at[e, s])
        wait_bytes(cost_b, send_sem.at[6, 0])
        wait_bytes(parts, send_sem.at[6, 1])

    return kernel


def solution(mesh):
    ny, nx = mesh.shape['qy'], mesh.shape['qx']
    n = ny * nx

    def device_fn(cost, gamma, beta):
        size = cost.shape[0]
        num_sets, num_layers = gamma.shape
        rows = size // (LANE * n)
        bits = (size * n).bit_length() - 1
        norm = 2.0 ** (-0.5 * bits)
        state = (n, rows, 2 * LANE)
        smem = pl.BlockSpec(memory_space=pltpu.SMEM)
        energy, grad = pl.pallas_call(
            make_kernel(ny, nx, num_sets, num_layers, rows, norm),
            out_shape=(jax.ShapeDtypeStruct((num_sets,), F32), jax.ShapeDtypeStruct((num_sets, 2 * num_layers), F32)),
            in_specs=[pl.BlockSpec(memory_space=pltpu.VMEM), smem, smem],
            out_specs=(smem, smem),
            scratch_shapes=[
                pltpu.VMEM((n, rows, LANE), F32),
                pltpu.VMEM((6, num_sets) + state, F32),
                pltpu.VMEM((6, num_sets) + state, F32),
                pltpu.VMEM((11, num_sets) + state, F32),
                pltpu.VMEM((2, num_sets) + state, F32),
                pltpu.VMEM((num_sets,) + state, F32),
                pltpu.VMEM((num_sets,) + state, F32),
                pltpu.VMEM((num_sets * num_layers, 2, 3, 2 * LANE, 2 * LANE), BF16),
                pltpu.VMEM((2 * LANE, 2 * LANE), BF16),
                pltpu.VMEM((LANE, LANE), jnp.int32),
                pltpu.VMEM((num_sets * num_layers, 3, SUB, LANE), F32),
                pltpu.VMEM((num_sets * 8, SUB, LANE), F32),
                pltpu.VMEM((1, SUB, LANE), F32),
                pltpu.VMEM((n, SUB, LANE), F32),
                pltpu.VMEM(state, F32),
                pltpu.SemaphoreType.DMA((7, 2)),
                pltpu.SemaphoreType.DMA((7, 2)),
            ],
            compiler_params=pltpu.CompilerParams(collective_id=0, has_side_effects=True, vmem_limit_bytes=60 * 2 ** 20),
            name='qaoa',
        )(cost.reshape(n, rows, LANE), gamma, beta)
        return energy, grad

    cost_spec = P(('inst', 'qy', 'qx'))
    angle_spec = P('inst', None)
    return jax.shard_map(device_fn, mesh=mesh, in_specs=(cost_spec, angle_spec, angle_spec), out_specs=(P('inst'), angle_spec), check_vma=False)
```

time: 1750 us -> 105 us (0.06)
  waiting for transfers between devices: 809 us -> 0 us
  other arithmetic: 502 us -> 0 us
  local copies, waits for them, and re-layouts: 308 us -> 1.85 us
  Pallas kernels: 0 us -> 103 us
  starting transfers between devices: 66.7 us -> 0 us
  blocking collectives: 48.5 us -> 0 us
    ppermute x30 -> x0, waiting for transfers between devices: 809 us -> none  [the longest x15 543 us: device_fn(): partner = lax.ppermute(jnp.stack(list(four_amps)), axis_name, pair_list)]
    concatenate x188 -> x0, local copies, waits for them, and re-layouts: 228 us -> none  [the longest x129 154 us: flip_grid(): jnp.roll(amplitudes, shift, axis=axis_pos)]
    add x70 -> x0, other arithmetic: 154 us -> none  [the longest x27 124 us: device_fn(): cos_b * psi_re + sin_b * flip_im]
    mul x29 -> x0, other arithmetic: 134 us -> none  [the longest x7 39.6 us: device_fn(): sin_b * flip_im]
    sub x51 -> x0, other arithmetic: 119 us -> none  [the longest x26 107 us: device_fn(): cos_b * psi_im - sin_b * flip_re]
    pallas_call x0 -> x1, Pallas kernels: none -> 103 us  [device_fn(): pl.pallas_call(make_kernel(ny, nx, num_sets, num_layers, rows, norm), out...]
    reduce_sum x62 -> x0, other arithmetic: 79.4 us -> none  [the longest x61 78 us: inverse_step(): term = jnp.sum(lam_re * partner[1] - lam_im * partner[0], axis=(1, 2))]
    slice x413 -> x0, local copies, waits for them, and re-layouts: 69.3 us -> none  [the longest x387 51.8 us: flip_grid(): jnp.roll(amplitudes, shift, axis=axis_pos)]
  transfers between devices with their start and end apart: 30 -> 0, of which waited for: 30 -> 0; matrix products, arithmetic and copies ran while one was open for 0% -> 0% of each run, Pallas kernels for 0% -> 0%
where the time goes in v1:
time: 105 us
  Pallas kernels  103 us (98%)
  local copies, waits for them, and re-layouts  1.85 us (2%)
    pallas_call x1, Pallas kernels, device_fn(): pl.pallas_call(make_kernel(ny, nx, num_sets, num_layers, rows, norm), out...  103 us

profile of v1, /device:TPU:97, one launch (start us, length us, event | category | flops | bytes accessed | tf_op | source)
XLA Modules:
  0.0 105.0 jit_solution(281082940349520925)
XLA Ops:
  0.6 102.5 %qaoa.1 = (f32[2]{0:T(128)}, f32[2,6]{1,0:T(2,128)}) custom-call(f32[32,16,128]{2,1,0:T(8,128)} %bitcast.1, f32[2,3]{1,0:T(2,128)} %gamma_ref.1, f32[2,3]{1,0:T(2,128)} %beta_ref.1), custom_call_target="tpu_custom_call" | custom-call | tf_op jit(solution)/shard_map/qaoa/pallas_call | solution.py:552
  103.2 0.0 copy-start.1
  103.2 0.6 copy-done.1
  103.8 0.0 copy-start
  103.8 0.5 copy.7
  104.3 0.2 copy-done
  104.5 0.6 copy.8
Async XLA Ops:
  103.2 0.6 copy-start.1
  103.8 0.7 copy-start

commit v2 on v1

--- a/solution.py
+++ b/solution.py
@@ -71,23 +71,27 @@
     tile_bits = [1 << b for b in range(tiles.bit_length() - 1)]
     width_x = nx // 2
 
-    def order(a):
-        return 2 - a + (a // 2) * (7 - 2 * a)
-
-    def kernel(cost_ref, gamma_ref, beta_ref, e_ref, g_ref,
-               cost_b, src, dst, keep, tab, psi_b, psi_c, wmat, adj, dmat, ct, acc, mine, parts, tmp, send_sem, recv_sem):
+    def kernel(cost_ref, gamma_ref, beta_ref, parts,
+               cost_b, src, dst, keep, tab, psi_b, psi_c, wmat, adj, dmat, ct, acc, mine, tmp, send_sem, recv_sem):
         qy = lax.axis_index('qy')
         qx = lax.axis_index('qx')
         me = qy * nx + qx
         barrier = pltpu.get_barrier_semaphore()
 
+        chip_x = [lax.rem(qx // 2 + dx, width_x) * 2 for dx in (1, 3, 2, 0)]
+
         def each_peer(act):
             def body(i, _):
-                ty = lax.rem(qy + order(i // (2 * width_x)), ny)
-                tx = lax.rem(qx // 2 + order(lax.rem(i // 2, width_x)), width_x) * 2 + lax.rem(qx + 1 + i, 2)
-                act(ty, tx)
-                return 0
-            lax.fori_loop(0, n - 1, body, 0)
+                ty = lax.rem(qy + 1 + i, ny)
+                core = lax.rem(qx + 1 + i // ny, 2)
+                for tx in chip_x[:-1]:
+                    act(ty, tx + core)
+
+                @pl.when(i < 2 * ny - 1)
+                def _():
+                    act(ty, chip_x[-1] + core)
+                return 0
+            lax.fori_loop(0, 2 * ny, body, 0)
 
         def greet(ty, tx):
             pl.semaphore_signal(barrier, inc=1, device_id={'qy': ty, 'qx': tx}, device_id_type=MESH_ID)
@@ -250,14 +254,17 @@
             lax.fori_loop(0, hi, rows_body, 0)
 
             def lanes_body(i, _):
-                at = pl.ds(pl.multiple_of(i * lo, lo), lo)
-                x = tmp[at].reshape(lo * rows, 2 * LANE)
+                at = pl.ds(pl.multiple_of(i * 16, 16), 16)
+                m = 16 * rows
+                x = tmp[at].reshape(m, 2 * LANE)
                 xh, xm, xl = split3(x)
                 w = [wmat[k, sign - 1, p] for p in range(3)]
-                y = mm(xh, w[0]) + (mm(xh, w[1]) + mm(xm, w[0])) + (mm(xh, w[2]) + mm(xm, w[1]) + mm(xl, w[0]))
-                target[at] = y.reshape(lo, rows, 2 * LANE)
-                return 0
-            lax.fori_loop(0, hi, lanes_body, 0)
+                a = mm(jnp.concatenate([xh, xm, xl], axis=0), w[0])
+                b = mm(jnp.concatenate([xh, xm], axis=0), w[1])
+                y = a[:m] + (b[:m] + a[m:2 * m]) + (mm(xh, w[2]) + b[m:] + a[2 * m:])
+                target[at] = y.reshape(16, rows, 2 * LANE)
+                return 0
+            lax.fori_loop(0, n // 16, lanes_body, 0)
 
         def im_dot(a, b):
             return a[0] * b[1] - a[1] * b[0]
@@ -401,33 +408,33 @@
             acc[row] = a if init else acc[row] + a
 
 
-        def set_weights(k, _):
-            weights(k, k)
-            return 0
-        lax.fori_loop(0, num_sets * num_layers, set_weights, 0)
-        pl.semaphore_wait(barrier, n - 1)
-        exchange(cost_ref, cost_b, (6, 0))
-
         def each_set(f):
             lax.fori_loop(0, num_sets, lambda s, _: (f(s), 0)[1], 0)
 
-        cost_b[me] = cost_ref[me]
-
-        @each_set
-        def _(s):
+        def first_layer(s):
+            weights(kk(s, 0), kk(s, 0))
             fill_table(keep.at[0, s], cost_ref, s, 0, norm)
             mid_pass(keep.at[0, s], tmp, None, 1, kk(s, 0), 1, lambda v, slots, tile, a: (v, a))
             pre_mix(tmp, src.at[0, s], kk(s, 0), 1)
             own(src.at[0, s], dst.at[0, s])
+
+        first_layer(0)
+        pl.semaphore_wait(barrier, n - 1)
+        exchange(src.at[0, 0], dst.at[0, 0], (0, 0))
+        exchange(cost_ref, cost_b, (6, 0))
+        cost_b[me] = cost_ref[me]
+        for s in range(1, num_sets):
+            first_layer(s)
             exchange(src.at[0, s], dst.at[0, s], (0, s))
 
+        def set_weights(i, _):
+            k = (i // (num_layers - 1)) * num_layers + 1 + i % (num_layers - 1)
+            weights(k, k)
+            return 0
+        lax.fori_loop(0, num_sets * (num_layers - 1), set_weights, 0)
+        each_set(lambda s: fill_table(tab.at[1, s], cost_ref, s, 2, None))
         wait_bytes(cost_b, recv_sem.at[6, 0])
-        @each_set
-        def _(s):
-            fill_table(tab.at[0, s], cost_b, s, 1, None)
-        @each_set
-        def _(s):
-            fill_table(tab.at[1, s], cost_ref, s, 2, None)
+        each_set(lambda s: fill_table(tab.at[0, s], cost_b, s, 1, None))
 
         def forward_mid(before, after, table):
             def middle(v, slots, tile, a):
@@ -511,23 +518,15 @@
             add_acc(s, 1, 2.0 * g, True)
 
         lane = lax.broadcasted_iota(jnp.int32, (1, LANE), 1)
-        vec = jnp.zeros((1, LANE), F32)
         for s in range(num_sets):
+            vec = jnp.zeros((1, LANE), F32)
             for q in range(1 + 2 * num_layers):
                 total = jnp.sum(jnp.sum(acc[s * 8 + q], axis=0, keepdims=True), axis=1, keepdims=True)
-                vec = jnp.where(lane == s * 8 + q, total, vec)
-        mine[0] = jnp.broadcast_to(vec, (SUB, LANE))
-        parts[me] = jnp.broadcast_to(vec, (SUB, LANE))
-        each_peer(lambda ty, tx: send(mine.at[0], parts.at[me], (6, 1), ty, tx))
+                vec = jnp.where(lane == q, total, vec)
+            mine[s:s + 1, :] = vec
+        parts[me] = mine[...]
+        each_peer(lambda ty, tx: send(mine, parts.at[me], (6, 1), ty, tx))
         wait_bytes(parts, recv_sem.at[6, 1])
-        total = parts[0]
-        for m in range(1, n):
-            total = total + parts[m]
-        for s in range(num_sets):
-            e_ref[s] = total[0, s * 8]
-            for q in range(2 * num_layers):
-                g_ref[s, q] = total[0, s * 8 + 1 + q]
-
         for e in range(6):
             for s in range(num_sets):
                 wait_bytes(src.at[e, s], send_sem.at[e, s])
@@ -549,11 +548,11 @@
         norm = 2.0 ** (-0.5 * bits)
         state = (n, rows, 2 * LANE)
         smem = pl.BlockSpec(memory_space=pltpu.SMEM)
-        energy, grad = pl.pallas_call(
+        parts = pl.pallas_call(
             make_kernel(ny, nx, num_sets, num_layers, rows, norm),
-            out_shape=(jax.ShapeDtypeStruct((num_sets,), F32), jax.ShapeDtypeStruct((num_sets, 2 * num_layers), F32)),
+            out_shape=jax.ShapeDtypeStruct((n, num_sets, LANE), F32),
             in_specs=[pl.BlockSpec(memory_space=pltpu.VMEM), smem, smem],
-            out_specs=(smem, smem),
+            out_specs=pl.BlockSpec(memory_space=pltpu.VMEM),
             scratch_shapes=[
                 pltpu.VMEM((n, rows, LANE), F32),
                 pltpu.VMEM((6, num_sets) + state, F32),
@@ -567,8 +566,7 @@
                 pltpu.VMEM((LANE, LANE), jnp.int32),
                 pltpu.VMEM((num_sets * num_layers, 3, SUB, LANE), F32),
                 pltpu.VMEM((num_sets * 8, SUB, LANE), F32),
-                pltpu.VMEM((1, SUB, LANE), F32),
-                pltpu.VMEM((n, SUB, LANE), F32),
+                pltpu.VMEM((num_sets, LANE), F32),
                 pltpu.VMEM(state, F32),
                 pltpu.SemaphoreType.DMA((7, 2)),
                 pltpu.SemaphoreType.DMA((7, 2)),
@@ -576,7 +574,20 @@
             compiler_params=pltpu.CompilerParams(collective_id=0, has_side_effects=True, vmem_limit_bytes=60 * 2 ** 20),
             name='qaoa',
         )(cost.reshape(n, rows, LANE), gamma, beta)
-        return energy, grad
+
+        def finish(parts_ref, e_ref, g_ref):
+            total = jnp.sum(parts_ref[...], axis=0)
+            g_ref[...] = total[:, 1:1 + 2 * num_layers]
+            for s in range(num_sets):
+                e_ref[s] = total[s, 0]
+
+        return pl.pallas_call(
+            finish,
+            out_shape=(jax.ShapeDtypeStruct((num_sets,), F32), jax.ShapeDtypeStruct((num_sets, 2 * num_layers), F32)),
+            in_specs=[pl.BlockSpec(memory_space=pltpu.VMEM)],
+            out_specs=(smem, pl.BlockSpec(memory_space=pltpu.VMEM)),
+            name='finish',
+        )(parts)
 
     cost_spec = P(('inst', 'qy', 'qx'))
     angle_spec = P('inst', None)

time: 105 us -> 95.3 us (0.908)
  Pallas kernels: 103 us -> 94.5 us
  local copies, waits for them, and re-layouts: 1.85 us -> 0 us
    pallas_call x1, Pallas kernels: 103 us -> 93.1 us  [device_fn(): pl.pallas_call(make_kernel(ny, nx, num_sets, num_layers, rows, norm), out...]
    unnamed x6 -> x0, local copies, waits for them, and re-layouts: 1.85 us -> none
    pallas_call x0 -> x1, Pallas kernels: none -> 1.43 us  [device_fn(): pl.pallas_call(finish, out_shape=(jax.ShapeDtypeStruct((num_sets,), F32),...]
where the time goes in v2:
time: 95.3 us; the launch traced here: 95.1 us
  Pallas kernels  94.5 us (99%)
    pallas_call x1, Pallas kernels, device_fn(): pl.pallas_call(make_kernel(ny, nx, num_sets, num_layers, rows, norm), out...  93.1 us

profile of v2, /device:TPU:97, one launch (start us, length us, event | category | flops | bytes accessed | tf_op | source)
XLA Modules:
  0.0 95.1 jit_solution(11904367892822178976)
XLA Ops:
  0.6 93.1 %qaoa.1.parts_ref = f32[32,2,128]{2,1,0:T(2,128)} custom-call(f32[32,16,128]{2,1,0:T(8,128)} %bitcast.1, f32[2,3]{1,0:T(2,128)} %gamma_ref.1, f32[2,3]{1,0:T(2,128)} %beta_ref.1), custom_call_target="tpu_custom_call" | custom-call | tf_op jit(solution)/shard_map/qaoa/pallas_call | solution.py:551
  93.7 1.4 %finish.1 = (f32[2]{0:T(128)}, f32[2,6]{1,0:T(2,128)}) custom-call(f32[32,2,128]{2,1,0:T(2,128)} %qaoa.1.parts_ref), custom_call_target="tpu_custom_call" | custom-call | tf_op jit(solution)/shard_map/finish/pallas_call | solution.py:584

commit v3 on v2

--- a/solution.py
+++ b/solution.py
@@ -9,6 +9,8 @@
 LANE = 128
 LANE_BITS = 7
 SUB = 8
+ORDER_OTHER = [(dy, dx) for dy in (1, 2, 3, 0) for dx in (1, 3, 2, 0)]
+ORDER_LIKE = ORDER_OTHER[:-1]
 MESH_ID = pl.DeviceIdType.MESH
 F32 = jnp.float32
 BF16 = jnp.bfloat16
@@ -72,38 +74,66 @@
     width_x = nx // 2
 
     def kernel(cost_ref, gamma_ref, beta_ref, parts,
-               cost_b, src, dst, keep, tab, psi_b, psi_c, wmat, adj, dmat, ct, acc, mine, tmp, send_sem, recv_sem):
+               cost_b, src, dst, keep, tab, psi_b, psi_c, wmat, adj, dmat, ct, acc, mine, tmp, other, send_sem, recv_sem):
         qy = lax.axis_index('qy')
         qx = lax.axis_index('qx')
         me = qy * nx + qx
         barrier = pltpu.get_barrier_semaphore()
 
-        chip_x = [lax.rem(qx // 2 + dx, width_x) * 2 for dx in (1, 3, 2, 0)]
-
-        def each_peer(act):
+        me_core = lax.rem(qx, 2)
+
+        def ring_x(order):
+            return [lax.rem(qx // 2 + dx, width_x) * 2 for dx in order]
+        chip_x = ring_x((1, 3, 2, 0))
+        far_x = ring_x((2, 1, 3, 0))
+
+        def peers_of_core(act, core, last):
             def body(i, _):
                 ty = lax.rem(qy + 1 + i, ny)
-                core = lax.rem(qx + 1 + i // ny, 2)
                 for tx in chip_x[:-1]:
                     act(ty, tx + core)
 
+                @pl.when(i + last < ny)
+                def _():
+                    act(ty, chip_x[-1] + core)
+                return 0
+            lax.fori_loop(0, ny, body, 0)
+
+        def peers_in_order(act, order, core):
+            for dy, dx in order:
+                act(lax.rem(qy + dy, ny), lax.rem(qx // 2 + dx, width_x) * 2 + core)
+
+        def both_cores(f):
+            lax.fori_loop(0, 2, lambda h, _: (f(lax.rem(me_core + 1 + h, 2), h), 0)[1], 0)
+
+        def each_peer(act):
+            both_cores(lambda core, last: peers_of_core(act, core, last))
+
+        def each_peer_far_first(act):
+            def body(i, _):
+                a = i // 2
+                ty = lax.rem(qy + 2 - a + (a // 2) * (7 - 2 * a), ny)
+                core = lax.rem(qx + 1 + i, 2)
+                for tx in far_x[:-1]:
+                    act(ty, tx + core)
+
                 @pl.when(i < 2 * ny - 1)
                 def _():
-                    act(ty, chip_x[-1] + core)
+                    act(ty, far_x[-1] + core)
                 return 0
             lax.fori_loop(0, 2 * ny, body, 0)
 
         def greet(ty, tx):
             pl.semaphore_signal(barrier, inc=1, device_id={'qy': ty, 'qx': tx}, device_id_type=MESH_ID)
-        each_peer(greet)
+        each_peer_far_first(greet)
 
         def send(source, target, ids, ty, tx):
             pltpu.make_async_remote_copy(
                 source, target, send_sem.at[ids], recv_sem.at[ids],
                 device_id={'qy': ty, 'qx': tx}, device_id_type=MESH_ID).start()
 
-        def exchange(source, target, ids):
-            each_peer(lambda ty, tx: send(source.at[ty * nx + tx], target.at[me], ids, ty, tx))
+        def by_core(ty, tx):
+            return lax.rem(tx, 2) * (n // 2) + ty * width_x + tx // 2
 
         def wait_bytes(buf, sem):
             part = buf.at[pl.ds(0, n - 1)]
@@ -234,8 +264,9 @@
                 return carry
             return lax.fori_loop(0, lo * tiles, body, jnp.zeros((SUB, LANE), F32))
 
-        def pre_mix(source, target, k, sign):
+        def pre_mix_send(source, e, s, k, sign):
             c, t = ct[k, 0], ct[k, sign]
+            half = n // 2
 
             def rows_body(i, _):
                 base = i * lo
@@ -249,22 +280,30 @@
                     for b in range(3):
                         fr, fi = sub_flip(re, b), sub_flip(im, b)
                         re, im = c * re + t * fi, c * im - t * fr
-                    store(tmp, base + j // tiles, j % tiles, (re, im))
+                    m = j // tiles
+                    store(tmp, (m % 2) * half + i * (lo // 2) + m // 2, j % tiles, (re, im))
                 return 0
             lax.fori_loop(0, hi, rows_body, 0)
 
-            def lanes_body(i, _):
-                at = pl.ds(pl.multiple_of(i * 16, 16), 16)
-                m = 16 * rows
+            def lanes(core):
+                at = pl.ds(pl.multiple_of(core * half, half), half)
+                m = half * rows
                 x = tmp[at].reshape(m, 2 * LANE)
                 xh, xm, xl = split3(x)
                 w = [wmat[k, sign - 1, p] for p in range(3)]
                 a = mm(jnp.concatenate([xh, xm, xl], axis=0), w[0])
                 b = mm(jnp.concatenate([xh, xm], axis=0), w[1])
                 y = a[:m] + (b[:m] + a[m:2 * m]) + (mm(xh, w[2]) + b[m:] + a[2 * m:])
-                target[at] = y.reshape(16, rows, 2 * LANE)
-                return 0
-            lax.fori_loop(0, n // 16, lanes_body, 0)
+                src[e, s, at] = y.reshape(half, rows, 2 * LANE)
+
+            def send_slot(ty, tx):
+                send(src.at[e, s, by_core(ty, tx)], dst.at[e, s, me], (e, s), ty, tx)
+            other_core = lax.rem(me_core + 1, 2)
+            lanes(other_core)
+            peers_in_order(send_slot, ORDER_OTHER, other_core)
+            lanes(me_core)
+            peers_in_order(send_slot, ORDER_LIKE, me_core)
+            dst[e, s, me] = src[e, s, by_core(qy, qx)]
 
         def im_dot(a, b):
             return a[0] * b[1] - a[1] * b[0]
@@ -388,18 +427,6 @@
                 return 0
             lax.fori_loop(0, n, body, 0)
 
-        def own(source, target):
-            target[me] = source[me]
-
-        def stage(e, s, e_next, k_in, s_in, k_out, s_out, middle):
-            wait_bytes(dst.at[e, s], recv_sem.at[e, s])
-            mix_low(dst.at[e, s], tmp, k_in, s_in)
-            a = mid_pass(tmp, tmp, k_in, s_in, k_out, s_out, middle)
-            pre_mix(tmp, src.at[e_next, s], k_out, s_out)
-            own(src.at[e_next, s], dst.at[e_next, s])
-            exchange(src.at[e_next, s], dst.at[e_next, s], (e_next, s))
-            return a
-
         def kk(s, l):
             return s * num_layers + l
 
@@ -411,30 +438,19 @@
         def each_set(f):
             lax.fori_loop(0, num_sets, lambda s, _: (f(s), 0)[1], 0)
 
-        def first_layer(s):
+        def first_state(s):
             weights(kk(s, 0), kk(s, 0))
             fill_table(keep.at[0, s], cost_ref, s, 0, norm)
-            mid_pass(keep.at[0, s], tmp, None, 1, kk(s, 0), 1, lambda v, slots, tile, a: (v, a))
-            pre_mix(tmp, src.at[0, s], kk(s, 0), 1)
-            own(src.at[0, s], dst.at[0, s])
-
-        first_layer(0)
+
+        first_state(0)
         pl.semaphore_wait(barrier, n - 1)
-        exchange(src.at[0, 0], dst.at[0, 0], (0, 0))
-        exchange(cost_ref, cost_b, (6, 0))
+        each_peer(lambda ty, tx: send(cost_ref.at[ty * nx + tx], cost_b.at[me], (6, 0), ty, tx))
         cost_b[me] = cost_ref[me]
-        for s in range(1, num_sets):
-            first_layer(s)
-            exchange(src.at[0, s], dst.at[0, s], (0, s))
 
         def set_weights(i, _):
             k = (i // (num_layers - 1)) * num_layers + 1 + i % (num_layers - 1)
             weights(k, k)
             return 0
-        lax.fori_loop(0, num_sets * (num_layers - 1), set_weights, 0)
-        each_set(lambda s: fill_table(tab.at[1, s], cost_ref, s, 2, None))
-        wait_bytes(cost_b, recv_sem.at[6, 0])
-        each_set(lambda s: fill_table(tab.at[0, s], cost_b, s, 1, None))
 
         def forward_mid(before, after, table):
             def middle(v, slots, tile, a):
@@ -473,59 +489,102 @@
                 return out, a
             return middle
 
-        @each_set
-        def _(s):
-            stage(0, s, 1, kk(s, 0), 1, kk(s, 1), 1, forward_mid(keep.at[1, s], keep.at[2, s], tab.at[0, s]))
-        @each_set
-        def _(s):
-            stage(1, s, 2, kk(s, 1), 1, kk(s, 2), 1, forward_mid(keep.at[3, s], keep.at[4, s], tab.at[1, s]))
-            inner_apply(keep.at[0, s], psi_b.at[s])
-            slot_x(keep.at[0, s], psi_b.at[s])
-            slot_mix_all(psi_b.at[s], kk(s, 0))
-
-            def times_cost(i, _):
-                for j in range(tiles):
-                    re, im = load(keep.at[0, s], i, j)
-                    w = cost_ref[i, tile_rows(j), :]
-                    store(psi_c.at[s], i, j, (w * re, w * im))
-                return 0
-            lax.fori_loop(0, n, times_cost, 0)
-            slot_mix_all(psi_c.at[s], kk(s, 0))
-        @each_set
-        def _(s):
-            a = stage(2, s, 3, kk(s, 2), 1, kk(s, 2), 2, turn_mid(keep.at[5, s], keep.at[6, s]))
-            add_acc(s, 0, a, True)
-            add_acc(s, 6, slot_dot(keep.at[6, s], keep.at[5, s]), True)
-        @each_set
-        def _(s):
-            stage(3, s, 4, kk(s, 2), 2, kk(s, 1), 2, backward_mid(keep.at[7, s], keep.at[8, s], tab.at[1, s]))
-            b, g = inner_dots(keep.at[7, s], keep.at[4, s], cost_ref)
-            add_acc(s, 6, b + slot_dot(keep.at[7, s], keep.at[4, s]))
-            add_acc(s, 3, 2.0 * g, True)
-            add_acc(s, 5, slot_dot(keep.at[8, s], keep.at[3, s]), True)
-        @each_set
-        def _(s):
-            stage(4, s, 5, kk(s, 1), 2, kk(s, 0), 2, backward_mid(keep.at[9, s], keep.at[10, s], tab.at[0, s]))
-            b, g = inner_dots(keep.at[9, s], keep.at[2, s], cost_b)
-            add_acc(s, 5, b + slot_dot(keep.at[9, s], keep.at[2, s]))
-            add_acc(s, 2, 2.0 * g, True)
-            add_acc(s, 4, slot_dot(keep.at[10, s], keep.at[1, s]), True)
-        @each_set
-        def _(s):
+        def stage(e, s):
+            k_out = kk(s, e - (e // 3) * (2 * e - 5))
+            s_out = 1 + e // 3
+            k_in = kk(s, e - 1 - (e // 4) * (2 * e - 7))
+            s_in = 1 + e // 4
+            before, after = keep.at[2 * e - 1, s], keep.at[2 * e, s]
+
+            @pl.when(e == 0)
+            def _():
+                @pl.when(s > 0)
+                def _():
+                    first_state(s)
+                mid_pass(keep.at[0, s], other, None, 1, k_out, s_out, lambda v, slots, tile, a: (v, a))
+
+            @pl.when(e > 0)
+            def _():
+                wait_bytes(dst.at[e - 1, s], recv_sem.at[e - 1, s])
+                mix_low(dst.at[e - 1, s], other, k_in, s_in)
+
+                @pl.when(e < 3)
+                def _():
+                    mid_pass(other, other, k_in, s_in, k_out, s_out, forward_mid(before, after, tab.at[e - 1, s]))
+
+                @pl.when(e == 3)
+                def _():
+                    add_acc(s, 0, mid_pass(other, other, k_in, s_in, k_out, s_out, turn_mid(before, after)), True)
+
+                @pl.when(e > 3)
+                def _():
+                    mid_pass(other, other, k_in, s_in, k_out, s_out, backward_mid(before, after, tab.at[5 - e, s]))
+
+            pre_mix_send(other, e, s, k_out, s_out)
+
+            @pl.when(e * num_sets + s == 1)
+            def _():
+                lax.fori_loop(0, num_sets * (num_layers - 1), set_weights, 0)
+                each_set(lambda i: fill_table(tab.at[1, i], cost_ref, i, 2, None))
+                wait_bytes(cost_b, recv_sem.at[6, 0])
+                each_set(lambda i: fill_table(tab.at[0, i], cost_b, i, 1, None))
+
+            @pl.when(e == 2)
+            def _():
+                inner_apply(keep.at[0, s], psi_b.at[s])
+                slot_x(keep.at[0, s], psi_b.at[s])
+                slot_mix_all(psi_b.at[s], kk(s, 0))
+
+                def times_cost(i, _):
+                    for j in range(tiles):
+                        re, im = load(keep.at[0, s], i, j)
+                        w = cost_ref[i, tile_rows(j), :]
+                        store(psi_c.at[s], i, j, (w * re, w * im))
+                    return 0
+                lax.fori_loop(0, n, times_cost, 0)
+                slot_mix_all(psi_c.at[s], kk(s, 0))
+
+            @pl.when(e == 3)
+            def _():
+                add_acc(s, 6, slot_dot(after, before), True)
+
+            @pl.when(e > 3)
+            def _():
+                ket = keep.at[12 - 2 * e, s]
+                ket_before = keep.at[11 - 2 * e, s]
+
+                def add_dots(cost):
+                    b, g = inner_dots(before, ket, cost)
+                    acc[s * 8 + 10 - e] = acc[s * 8 + 10 - e] + (b + slot_dot(before, ket))
+                    acc[s * 8 + 7 - e] = 2.0 * g
+                    acc[s * 8 + 9 - e] = slot_dot(after, ket_before)
+                pl.when(e == 4)(lambda: add_dots(cost_ref))
+                pl.when(e == 5)(lambda: add_dots(cost_b))
+
+        def each_exchange(e, _):
+            each_set(lambda s: stage(e, s))
+            return 0
+        lax.fori_loop(0, 2 * num_layers, each_exchange, 0)
+
+        lane = lax.broadcasted_iota(jnp.int32, (1, LANE), 1)
+
+        def place(q, a):
+            total = jnp.sum(jnp.sum(a, axis=0, keepdims=True), axis=1, keepdims=True)
+            return jnp.where(lane == q, total, 0.0)
+
+        def partial(s):
             wait_bytes(dst.at[5, s], recv_sem.at[5, s])
             b, g = two_dots(dst.at[5, s], psi_b.at[s], psi_c.at[s])
-            add_acc(s, 4, b)
-            add_acc(s, 1, 2.0 * g, True)
-
-        lane = lax.broadcasted_iota(jnp.int32, (1, LANE), 1)
+            return place(4, acc[s * 8 + 4] + b) + place(1, 2.0 * g)
+
+        rest = []
         for s in range(num_sets):
-            vec = jnp.zeros((1, LANE), F32)
-            for q in range(1 + 2 * num_layers):
-                total = jnp.sum(jnp.sum(acc[s * 8 + q], axis=0, keepdims=True), axis=1, keepdims=True)
-                vec = jnp.where(lane == q, total, vec)
-            mine[s:s + 1, :] = vec
+            rest.append(sum(place(q, acc[s * 8 + q]) for q in (2, 3, 5, 6)) + place(0, acc[s * 8]))
+        for s in range(num_sets):
+            mine[s:s + 1, :] = rest[s] + partial(s)
+
         parts[me] = mine[...]
-        each_peer(lambda ty, tx: send(mine, parts.at[me], (6, 1), ty, tx))
+        each_peer_far_first(lambda ty, tx: send(mine, parts.at[me], (6, 1), ty, tx))
         wait_bytes(parts, recv_sem.at[6, 1])
         for e in range(6):
             for s in range(num_sets):
@@ -568,6 +627,7 @@
                 pltpu.VMEM((num_sets * 8, SUB, LANE), F32),
                 pltpu.VMEM((num_sets, LANE), F32),
                 pltpu.VMEM(state, F32),
+                pltpu.VMEM(state, F32),
                 pltpu.SemaphoreType.DMA((7, 2)),
                 pltpu.SemaphoreType.DMA((7, 2)),
             ],

time: 95.3 us -> 94.2 us (0.988)
  Pallas kernels: 94.5 us -> 93.4 us
    pallas_call x1, Pallas kernels: 93.1 us -> 92 us  [device_fn(): pl.pallas_call(make_kernel(ny, nx, num_sets, num_layers, rows, norm), out...]
where the time goes in v3:
time: 94.2 us; the launch traced here: 94.1 us
  Pallas kernels  93.4 us (99%)
    pallas_call x1, Pallas kernels, device_fn(): pl.pallas_call(make_kernel(ny, nx, num_sets, num_layers, rows, norm), out...  92 us

profile of v3, /device:TPU:97, one launch (start us, length us, event | category | flops | bytes accessed | tf_op | source)
XLA Modules:
  0.0 94.1 jit_solution(13191925529276419662)
XLA Ops:
  0.6 92.0 %qaoa.1.parts_ref = f32[32,2,128]{2,1,0:T(2,128)} custom-call(f32[32,16,128]{2,1,0:T(8,128)} %bitcast.1, f32[2,3]{1,0:T(2,128)} %gamma_ref.1, f32[2,3]{1,0:T(2,128)} %beta_ref.1), custom_call_target="tpu_custom_call" | custom-call | tf_op jit(solution)/shard_map/qaoa/pallas_call | solution.py:610
  92.6 1.4 %finish.1 = (f32[2]{0:T(128)}, f32[2,6]{1,0:T(2,128)}) custom-call(f32[32,2,128]{2,1,0:T(2,128)} %qaoa.1.parts_ref), custom_call_target="tpu_custom_call" | custom-call | tf_op jit(solution)/shard_map/finish/pallas_call | solution.py:644

commit v4 on v3

--- a/solution.py
+++ b/solution.py
@@ -9,8 +9,8 @@
 LANE = 128
 LANE_BITS = 7
 SUB = 8
-ORDER_OTHER = [(dy, dx) for dy in (1, 2, 3, 0) for dx in (1, 3, 2, 0)]
-ORDER_LIKE = ORDER_OTHER[:-1]
+ORDER_OTHER = [(1, 1), (1, 3), (1, 2), (1, 0), (2, 1), (2, 3), (2, 2), (2, 0), (3, 1), (3, 3), (3, 2), (3, 0), (0, 1), (0, 3), (0, 2), (0, 0)]
+ORDER_LIKE = [(1, 1), (1, 3), (1, 2), (1, 0), (2, 1), (2, 3), (2, 2), (2, 0), (3, 1), (3, 3), (3, 2), (3, 0), (0, 1), (0, 3), (0, 2)]
 MESH_ID = pl.DeviceIdType.MESH
 F32 = jnp.float32
 BF16 = jnp.bfloat16
@@ -100,8 +100,9 @@
             lax.fori_loop(0, ny, body, 0)
 
         def peers_in_order(act, order, core):
-            for dy, dx in order:
-                act(lax.rem(qy + dy, ny), lax.rem(qx // 2 + dx, width_x) * 2 + core)
+            for part in range(tiles):
+                for dy, dx in order:
+                    act(lax.rem(qy + dy, ny), lax.rem(qx // 2 + dx, width_x) * 2 + core, part)
 
         def both_cores(f):
             lax.fori_loop(0, 2, lambda h, _: (f(lax.rem(me_core + 1 + h, 2), h), 0)[1], 0)
@@ -296,12 +297,13 @@
                 y = a[:m] + (b[:m] + a[m:2 * m]) + (mm(xh, w[2]) + b[m:] + a[2 * m:])
                 src[e, s, at] = y.reshape(half, rows, 2 * LANE)
 
-            def send_slot(ty, tx):
-                send(src.at[e, s, by_core(ty, tx)], dst.at[e, s, me], (e, s), ty, tx)
+            def send_slot(ty, tx, part):
+                r = pl.ds(part * SUB, SUB)
+                send(src.at[e, s, by_core(ty, tx), r], dst.at[e, s, me, r], (e, s), ty, tx)
             other_core = lax.rem(me_core + 1, 2)
             lanes(other_core)
+            lanes(me_core)
             peers_in_order(send_slot, ORDER_OTHER, other_core)
-            lanes(me_core)
             peers_in_order(send_slot, ORDER_LIKE, me_core)
             dst[e, s, me] = src[e, s, by_core(qy, qx)]
 

time: 94.2 us -> 91.4 us (0.970)
  Pallas kernels: 93.4 us -> 90.6 us
    pallas_call x1, Pallas kernels: 92 us -> 89.2 us  [device_fn(): pl.pallas_call(make_kernel(ny, nx, num_sets, num_layers, rows, norm), out...]
where the time goes in v4:
time: 91.4 us; the launch traced here: 91.2 us
  Pallas kernels  90.6 us (99%)
    pallas_call x1, Pallas kernels, device_fn(): pl.pallas_call(make_kernel(ny, nx, num_sets, num_layers, rows, norm), out...  89.2 us

profile of v4, /device:TPU:97, one launch (start us, length us, event | category | flops | bytes accessed | tf_op | source)
XLA Modules:
  0.0 91.2 jit_solution(10900043195209460852)
XLA Ops:
  0.6 89.2 %qaoa.1.parts_ref = f32[32,2,128]{2,1,0:T(2,128)} custom-call(f32[32,16,128]{2,1,0:T(8,128)} %bitcast.1, f32[2,3]{1,0:T(2,128)} %gamma_ref.1, f32[2,3]{1,0:T(2,128)} %beta_ref.1), custom_call_target="tpu_custom_call" | custom-call | tf_op jit(solution)/shard_map/qaoa/pallas_call | solution.py:612
  89.8 1.4 %finish.1 = (f32[2]{0:T(128)}, f32[2,6]{1,0:T(2,128)}) custom-call(f32[32,2,128]{2,1,0:T(2,128)} %qaoa.1.parts_ref), custom_call_target="tpu_custom_call" | custom-call | tf_op jit(solution)/shard_map/finish/pallas_call | solution.py:646

commit v5 on v4

--- a/solution.py
+++ b/solution.py
@@ -9,8 +9,8 @@
 LANE = 128
 LANE_BITS = 7
 SUB = 8
-ORDER_OTHER = [(1, 1), (1, 3), (1, 2), (1, 0), (2, 1), (2, 3), (2, 2), (2, 0), (3, 1), (3, 3), (3, 2), (3, 0), (0, 1), (0, 3), (0, 2), (0, 0)]
-ORDER_LIKE = [(1, 1), (1, 3), (1, 2), (1, 0), (2, 1), (2, 3), (2, 2), (2, 0), (3, 1), (3, 3), (3, 2), (3, 0), (0, 1), (0, 3), (0, 2)]
+ORDER_OTHER = [(2, 1), (2, 3), (2, 2), (2, 0), (1, 1), (1, 3), (1, 2), (1, 0), (3, 1), (3, 3), (3, 2), (3, 0), (0, 1), (0, 3), (0, 2), (0, 0)]
+ORDER_LIKE = [(2, 1), (2, 3), (2, 2), (2, 0), (1, 1), (1, 3), (1, 2), (1, 0), (3, 1), (3, 3), (3, 2), (3, 0), (0, 1), (0, 3), (0, 2)]
 MESH_ID = pl.DeviceIdType.MESH
 F32 = jnp.float32
 BF16 = jnp.bfloat16
@@ -73,8 +73,8 @@
     tile_bits = [1 << b for b in range(tiles.bit_length() - 1)]
     width_x = nx // 2
 
-    def kernel(cost_ref, gamma_ref, beta_ref, parts,
-               cost_b, src, dst, keep, tab, psi_b, psi_c, wmat, adj, dmat, ct, acc, mine, tmp, other, send_sem, recv_sem):
+    def kernel(cost_ref, gamma_ref, beta_ref, out_ref,
+               cost_b, src, dst, keep, tab, psi_b, psi_c, wmat, adj, dmat, ct, acc, mine, parts, tmp, other, send_sem, recv_sem):
         qy = lax.axis_index('qy')
         qx = lax.axis_index('qx')
         me = qy * nx + qx
@@ -391,7 +391,7 @@
                     g = g + im_dot(x, load(ket_c, i, j))
                 return a, g
             z = jnp.zeros((SUB, LANE), F32)
-            return lax.fori_loop(0, n, body, (z, z))
+            return lax.fori_loop(0, n, body, (z, z), unroll=4)
 
         def slot_x(source, target):
             def low(i, _):
@@ -588,6 +588,7 @@
         parts[me] = mine[...]
         each_peer_far_first(lambda ty, tx: send(mine, parts.at[me], (6, 1), ty, tx))
         wait_bytes(parts, recv_sem.at[6, 1])
+        out_ref[...] = jnp.sum(parts[...], axis=0)
         for e in range(6):
             for s in range(num_sets):
                 wait_bytes(src.at[e, s], send_sem.at[e, s])
@@ -611,7 +612,7 @@
         smem = pl.BlockSpec(memory_space=pltpu.SMEM)
         parts = pl.pallas_call(
             make_kernel(ny, nx, num_sets, num_layers, rows, norm),
-            out_shape=jax.ShapeDtypeStruct((n, num_sets, LANE), F32),
+            out_shape=jax.ShapeDtypeStruct((num_sets, LANE), F32),
             in_specs=[pl.BlockSpec(memory_space=pltpu.VMEM), smem, smem],
             out_specs=pl.BlockSpec(memory_space=pltpu.VMEM),
             scratch_shapes=[
@@ -628,6 +629,7 @@
                 pltpu.VMEM((num_sets * num_layers, 3, SUB, LANE), F32),
                 pltpu.VMEM((num_sets * 8, SUB, LANE), F32),
                 pltpu.VMEM((num_sets, LANE), F32),
+                pltpu.VMEM((n, num_sets, LANE), F32),
                 pltpu.VMEM(state, F32),
                 pltpu.VMEM(state, F32),
                 pltpu.SemaphoreType.DMA((7, 2)),
@@ -638,7 +640,7 @@
         )(cost.reshape(n, rows, LANE), gamma, beta)
 
         def finish(parts_ref, e_ref, g_ref):
-            total = jnp.sum(parts_ref[...], axis=0)
+            total = parts_ref[...]
             g_ref[...] = total[:, 1:1 + 2 * num_layers]
             for s in range(num_sets):
                 e_ref[s] = total[s, 0]

time: 91.4 us -> 91 us (level)
  no operation moved by 1% of the time
where the time goes in v5:
time: 91 us; the launch traced here: 90.9 us
  Pallas kernels  90.3 us (99%)
    pallas_call x1, Pallas kernels, device_fn(): pl.pallas_call(make_kernel(ny, nx, num_sets, num_layers, rows, norm), out...  89 us

profile of v5, /device:TPU:97, one launch (start us, length us, event | category | flops | bytes accessed | tf_op | source)
XLA Modules:
  0.0 90.9 jit_solution(13999283606564137074)
XLA Ops:
  0.6 89.0 %qaoa.1.parts_ref = f32[2,128]{1,0:T(2,128)} custom-call(f32[32,16,128]{2,1,0:T(8,128)} %bitcast.1, f32[2,3]{1,0:T(2,128)} %gamma_ref.1, f32[2,3]{1,0:T(2,128)} %beta_ref.1), custom_call_target="tpu_custom_call" | custom-call | tf_op jit(solution)/shard_map/qaoa/pallas_call | solution.py:613
  89.6 1.3 %finish.1 = (f32[2]{0:T(128)}, f32[2,6]{1,0:T(2,128)}) custom-call(f32[2,128]{1,0:T(2,128)} %qaoa.1.parts_ref), custom_call_target="tpu_custom_call" | custom-call | tf_op jit(solution)/shard_map/finish/pallas_call | solution.py:648

commit v6 on v5

--- a/solution.py
+++ b/solution.py
@@ -9,8 +9,8 @@
 LANE = 128
 LANE_BITS = 7
 SUB = 8
-ORDER_OTHER = [(2, 1), (2, 3), (2, 2), (2, 0), (1, 1), (1, 3), (1, 2), (1, 0), (3, 1), (3, 3), (3, 2), (3, 0), (0, 1), (0, 3), (0, 2), (0, 0)]
-ORDER_LIKE = [(2, 1), (2, 3), (2, 2), (2, 0), (1, 1), (1, 3), (1, 2), (1, 0), (3, 1), (3, 3), (3, 2), (3, 0), (0, 1), (0, 3), (0, 2)]
+ORDER_OTHER = [(1, 1), (1, 3), (1, 2), (1, 0), (2, 1), (2, 3), (2, 2), (2, 0), (3, 1), (3, 3), (3, 2), (3, 0), (0, 1), (0, 3), (0, 2), (0, 0)]
+ORDER_LIKE = [(1, 1), (1, 3), (1, 2), (1, 0), (2, 1), (2, 3), (2, 2), (2, 0), (3, 1), (3, 3), (3, 2), (3, 0), (0, 1), (0, 3), (0, 2)]
 MESH_ID = pl.DeviceIdType.MESH
 F32 = jnp.float32
 BF16 = jnp.bfloat16
@@ -74,7 +74,7 @@
     width_x = nx // 2
 
     def kernel(cost_ref, gamma_ref, beta_ref, out_ref,
-               cost_b, src, dst, keep, tab, psi_b, psi_c, wmat, adj, dmat, ct, acc, mine, parts, tmp, other, send_sem, recv_sem):
+               cost_b, src, dst, keep, tab, psi_b, psi_c, wmat, adj, dmat, ct, acc, mine, parts, tmp, other, send_sem, recv_sem, row_sem):
         qy = lax.axis_index('qy')
         qx = lax.axis_index('qx')
         me = qy * nx + qx
@@ -126,7 +126,28 @@
 
         def greet(ty, tx):
             pl.semaphore_signal(barrier, inc=1, device_id={'qy': ty, 'qx': tx}, device_id_type=MESH_ID)
-        each_peer_far_first(greet)
+        def line_peers(act):
+            def row(i, _):
+                act(qy, lax.rem(qx + i, nx))
+                return 0
+            lax.fori_loop(1, nx, row, 0)
+
+            def column(i, _):
+                act(lax.rem(qy + i, ny), qx)
+                act(lax.rem(qy + i, ny), qx + 1 - 2 * me_core)
+                return 0
+            lax.fori_loop(1, ny, column, 0)
+
+        def cross_peers(act):
+            def body(i, _):
+                ty = lax.rem(qy + 1 + i // 2, ny)
+                core = lax.rem(qx + 1 + i, 2)
+                for dx in (1, 3, 2):
+                    act(ty, lax.rem(qx // 2 + dx, width_x) * 2 + core)
+                return 0
+            lax.fori_loop(0, 2 * (ny - 1), body, 0)
+
+        line_peers(greet)
 
         def send(source, target, ids, ty, tx):
             pltpu.make_async_remote_copy(
@@ -238,7 +259,7 @@
                 for j in range(lo):
                     store(target, base + j, tile, v[j])
                 return 0
-            lax.fori_loop(0, hi * tiles, body, 0)
+            lax.fori_loop(0, hi * tiles, body, 0, unroll=2)
 
         def mid_pass(source, target, k_in, s_in, k_out, s_out, middle):
             if k_in is not None:
@@ -263,7 +284,7 @@
                     for j in range(hi):
                         store(target, slots[j], tile, v[j])
                 return carry
-            return lax.fori_loop(0, lo * tiles, body, jnp.zeros((SUB, LANE), F32))
+            return lax.fori_loop(0, lo * tiles, body, jnp.zeros((SUB, LANE), F32), unroll=2)
 
         def pre_mix_send(source, e, s, k, sign):
             c, t = ct[k, 0], ct[k, sign]
@@ -303,8 +324,16 @@
             other_core = lax.rem(me_core + 1, 2)
             lanes(other_core)
             lanes(me_core)
-            peers_in_order(send_slot, ORDER_OTHER, other_core)
-            peers_in_order(send_slot, ORDER_LIKE, me_core)
+            def near(order, want):
+                return [o for o in order if (o[0] == 0 or o[1] == 0) == want]
+            peers_in_order(send_slot, near(ORDER_OTHER, True), other_core)
+            peers_in_order(send_slot, near(ORDER_LIKE, True), me_core)
+
+            @pl.when(e + s == 0)
+            def _():
+                hear_rows()
+            peers_in_order(send_slot, near(ORDER_OTHER, False), other_core)
+            peers_in_order(send_slot, near(ORDER_LIKE, False), me_core)
             dst[e, s, me] = src[e, s, by_core(qy, qx)]
 
         def im_dot(a, b):
@@ -445,9 +474,22 @@
             fill_table(keep.at[0, s], cost_ref, s, 0, norm)
 
         first_state(0)
-        pl.semaphore_wait(barrier, n - 1)
-        each_peer(lambda ty, tx: send(cost_ref.at[ty * nx + tx], cost_b.at[me], (6, 0), ty, tx))
+        pl.semaphore_wait(barrier, nx - 1 + 2 * (ny - 1))
+
+        def tell(i, _):
+            pl.semaphore_signal(row_sem, inc=1, device_id={'qy': lax.rem(qy + i, ny), 'qx': qx}, device_id_type=MESH_ID)
+            return 0
+        lax.fori_loop(1, ny, tell, 0)
+
+        def send_cost(ty, tx):
+            send(cost_ref.at[ty * nx + tx], cost_b.at[me], (6, 0), ty, tx)
+        line_peers(send_cost)
         cost_b[me] = cost_ref[me]
+
+        def hear_rows():
+            pl.semaphore_wait(row_sem, ny - 1)
+            cross_peers(send_cost)
+
 
         def set_weights(i, _):
             k = (i // (num_layers - 1)) * num_layers + 1 + i % (num_layers - 1)
@@ -634,6 +676,7 @@
                 pltpu.VMEM(state, F32),
                 pltpu.SemaphoreType.DMA((7, 2)),
                 pltpu.SemaphoreType.DMA((7, 2)),
+                pltpu.SemaphoreType.REGULAR,
             ],
             compiler_params=pltpu.CompilerParams(collective_id=0, has_side_effects=True, vmem_limit_bytes=60 * 2 ** 20),
             name='qaoa',

time: 91 us -> 90.5 us (level)
  no operation moved by 1% of the time
where the time goes in v6:
time: 90.5 us; the launch traced here: 90.4 us
  Pallas kernels  89.7 us (99%)
    pallas_call x1, Pallas kernels, device_fn(): pl.pallas_call(make_kernel(ny, nx, num_sets, num_layers, rows, norm), out...  88.4 us

profile of v6, /device:TPU:97, one launch (start us, length us, event | category | flops | bytes accessed | tf_op | source)
XLA Modules:
  0.0 90.4 jit_solution(6607690597312966795)
XLA Ops:
  0.6 88.4 %qaoa.1.parts_ref = f32[2,128]{1,0:T(2,128)} custom-call(f32[32,16,128]{2,1,0:T(8,128)} %bitcast.1, f32[2,3]{1,0:T(2,128)} %gamma_ref.1, f32[2,3]{1,0:T(2,128)} %beta_ref.1), custom_call_target="tpu_custom_call" | custom-call | tf_op jit(solution)/shard_map/qaoa/pallas_call | solution.py:655
  89.0 1.3 %finish.1 = (f32[2]{0:T(128)}, f32[2,6]{1,0:T(2,128)}) custom-call(f32[2,128]{1,0:T(2,128)} %qaoa.1.parts_ref), custom_call_target="tpu_custom_call" | custom-call | tf_op jit(solution)/shard_map/finish/pallas_call | solution.py:691

commit v7 on v6

--- a/solution.py
+++ b/solution.py
@@ -420,7 +420,7 @@
                     g = g + im_dot(x, load(ket_c, i, j))
                 return a, g
             z = jnp.zeros((SUB, LANE), F32)
-            return lax.fori_loop(0, n, body, (z, z), unroll=4)
+            return lax.fori_loop(0, n, body, (z, z), unroll=8)
 
         def slot_x(source, target):
             def low(i, _):
@@ -683,16 +683,16 @@
         )(cost.reshape(n, rows, LANE), gamma, beta)
 
         def finish(parts_ref, e_ref, g_ref):
-            total = parts_ref[...]
-            g_ref[...] = total[:, 1:1 + 2 * num_layers]
             for s in range(num_sets):
-                e_ref[s] = total[s, 0]
+                e_ref[s] = parts_ref[s, 0]
+                for q in range(2 * num_layers):
+                    g_ref[s, q] = parts_ref[s, 1 + q]
 
         return pl.pallas_call(
             finish,
             out_shape=(jax.ShapeDtypeStruct((num_sets,), F32), jax.ShapeDtypeStruct((num_sets, 2 * num_layers), F32)),
-            in_specs=[pl.BlockSpec(memory_space=pltpu.VMEM)],
-            out_specs=(smem, pl.BlockSpec(memory_space=pltpu.VMEM)),
+            in_specs=[smem],
+            out_specs=(smem, smem),
             name='finish',
         )(parts)
 

time: 90.5 us -> 90.4 us (level)
  no operation moved by 1% of the time
where the time goes in v7:
time: 90.4 us; the launch traced here: 90.3 us
  Pallas kernels  89.7 us (99%)
    pallas_call x1, Pallas kernels, device_fn(): pl.pallas_call(make_kernel(ny, nx, num_sets, num_layers, rows, norm), out...  88.4 us

profile of v7, /device:TPU:97, one launch (start us, length us, event | category | flops | bytes accessed | tf_op | source)
XLA Modules:
  0.0 90.3 jit_solution(7581118669061826387)
XLA Ops:
  0.6 88.4 %qaoa.1.parts_ref = f32[2,128]{1,0:T(2,128)} custom-call(f32[32,16,128]{2,1,0:T(8,128)} %bitcast.1, f32[2,3]{1,0:T(2,128)} %gamma_ref.1, f32[2,3]{1,0:T(2,128)} %beta_ref.1), custom_call_target="tpu_custom_call" | custom-call | tf_op jit(solution)/shard_map/qaoa/pallas_call | solution.py:655
  89.0 1.3 %finish.1 = (f32[2]{0:T(128)}, f32[2,6]{1,0:T(2,128)}) custom-call(f32[2,128]{1,0:T(2,128)} %qaoa.1.parts_ref), custom_call_target="tpu_custom_call" | custom-call | tf_op jit(solution)/shard_map/finish/pallas_call | solution.py:691

commit v8 on v7

--- a/solution.py
+++ b/solution.py
@@ -629,12 +629,12 @@
 
         parts[me] = mine[...]
         each_peer_far_first(lambda ty, tx: send(mine, parts.at[me], (6, 1), ty, tx))
-        wait_bytes(parts, recv_sem.at[6, 1])
-        out_ref[...] = jnp.sum(parts[...], axis=0)
         for e in range(6):
             for s in range(num_sets):
                 wait_bytes(src.at[e, s], send_sem.at[e, s])
         wait_bytes(cost_b, send_sem.at[6, 0])
+        wait_bytes(parts, recv_sem.at[6, 1])
+        out_ref[...] = jnp.sum(parts[...], axis=0)
         wait_bytes(parts, send_sem.at[6, 1])
 
     return kernel

time: 90.4 us -> 90.4 us (level)
  no operation moved by 1% of the time
where the time goes in v8:
time: 90.4 us; the launch traced here: 90.3 us
  Pallas kernels  89.6 us (99%)
    pallas_call x1, Pallas kernels, device_fn(): pl.pallas_call(make_kernel(ny, nx, num_sets, num_layers, rows, norm), out...  88.4 us

profile of v8, /device:TPU:97, one launch (start us, length us, event | category | flops | bytes accessed | tf_op | source)
XLA Modules:
  0.0 90.3 jit_solution(11309689810834211184)
XLA Ops:
  0.6 88.4 %qaoa.1.parts_ref = f32[2,128]{1,0:T(2,128)} custom-call(f32[32,16,128]{2,1,0:T(8,128)} %bitcast.1, f32[2,3]{1,0:T(2,128)} %gamma_ref.1, f32[2,3]{1,0:T(2,128)} %beta_ref.1), custom_call_target="tpu_custom_call" | custom-call | tf_op jit(solution)/shard_map/qaoa/pallas_call | solution.py:655
  89.0 1.3 %finish.1 = (f32[2]{0:T(128)}, f32[2,6]{1,0:T(2,128)}) custom-call(f32[2,128]{1,0:T(2,128)} %qaoa.1.parts_ref), custom_call_target="tpu_custom_call" | custom-call | tf_op jit(solution)/shard_map/finish/pallas_call | solution.py:691
